TPU v7x, 32 devices: a whole 2x2x4 slice. The times are simulated.
32 devices in a mesh: lon: 8 (over z, x), lat: 4 (over y, core).
Axes of the slice: x: 2, y: 2, z: 4, core: 2. Of those that a mesh axis runs over, the one named last changes fastest.
Arguments:
- thermal_anomaly: float32 [32, 64, 512], P(None, 'lon', 'lat'), may hold values from -5 to 5
- saltiness_anomaly: float32 [32, 64, 512], P(None, 'lon', 'lat'), may hold values from -5 to 5
- zonal_flow: float32 [32, 64, 512], P(None, 'lon', 'lat'), may hold values from -1.2 to 1.2
- meridional_flow: float32 [32, 64, 512], P(None, 'lon', 'lat'), may hold values from -1.2 to 1.2
- submerged_strata_number: int32 [64, 512], P('lon', 'lat'), may hold values from 1 to 32
- sea_indicator: int32 [64, 512], P('lon', 'lat'), may hold values 0 or 1
- strata_thickness: float32 [32], replicated, may hold values from 0.5 to 2
- earlier_sea_elevation: float32 [64, 512], P('lon', 'lat'), may hold values from -3 to 3
- sea_drive_term: float32 [64, 512], P('lon', 'lat'), may hold values from -10 to 10
Outputs:
- new_temperature: float32 [32, 64, 512], P(None, 'lon', 'lat')
- new_salinity: float32 [32, 64, 512], P(None, 'lon', 'lat')
- new_u_velocity: float32 [32, 64, 512], P(None, 'lon', 'lat')
- new_v_velocity: float32 [32, 64, 512], P(None, 'lon', 'lat')
- new_surface: float32 [64, 512], P('lon', 'lat')
- residual_rms: float32 [], replicated
All inputs are finite; a program needn't handle non-finite values. No bound on the sum of `sea_indicator` on one device may be relied on, other than what follows from the above.
Results may differ from a plain program's by a relative error of at most 0.0003.
Values sent between devices are 32-bit elements; how exact they have to be, the bound alone decides.
A program may use at most 128 MiB of HBM per device.

v0:
```python
import functools

import jax
import jax.numpy as jnp
from jax import lax
from jax.experimental import pallas as pl
from jax.experimental.pallas import tpu as pltpu
from jax.sharding import PartitionSpec as P

ITERS = 4
DIFFUSION = 0.15
MIXING = 0.1
EXPANSION = 0.2
CONTRACTION = 0.15
PRESSURE_SCALE = 0.02
CORIOLIS = 0.5
FRICTION = 0.01
DIVERGENCE = 0.3
STORAGE = 0.1
SPECTRUM_LOW = 0.1
SPECTRUM_HIGH = 1.9
GRAVITY = 0.3
EPSILON = 1e-06

MESH = pl.DeviceIdType.MESH
F32 = jnp.float32
SLOT_N, SLOT_NE, SLOT_NW, SLOT_S, SLOT_SE, SLOT_SW = range(6)
SEM_E, SEM_W = 6, 7
EARLY = 3
LATE = 2


def iota(shape, axis):
    return lax.broadcasted_iota(jnp.int32, shape, axis)


def flip_rows(x):
    n = x.shape[0]
    row = iota(x.shape, 0)
    bit = n // 2
    while bit:
        up = pltpu.roll(x, bit, 0)
        down = pltpu.roll(x, n - bit, 0)
        x = up if 2 * bit == n else jnp.where((row & bit) != 0, up, down)
        bit //= 2
    return x


def step_kernel(n_lon, n_lat, KC, *refs):
    sources, refs = refs[:9], refs[9:]
    (ot_ref, os_ref, ou_ref, ov_ref, ox_ref), refs = refs[:5], refs[5:]
    inputs, refs = refs[:9], refs[9:]
    t_ref, s_ref, u_ref, v_ref, num_ref, sea_ref, thick_ref, eta_ref, drive_ref = inputs
    (epk, wpk, ebase, wbase, npk, spk, slot_e, slot_w, base_e, base_w, slots, rim, early, late, held,
     load_sem, send_sem, recv_sem, side_send, side_recv, cast_send, cast_recv) = refs
    K, NI, NJ = t_ref.shape
    NC = K // KC
    loads = [pltpu.make_async_copy(src, dst, load_sem.at[i]) for i, (src, dst) in enumerate(zip(sources, inputs))]
    for load in loads[4:] + loads[:4]:
        load.start()
    p = lax.axis_index("lon")
    q = lax.axis_index("lat")
    east_dev = lax.rem(p + 1, n_lon)
    west_dev = lax.rem(p + n_lon - 1, n_lon)
    at_pole = q == n_lat - 1
    not_pole = q < n_lat - 1
    not_south = q > 0
    mirror = n_lon - 1 - p
    mirror_ne = lax.rem(2 * n_lon - 2 - p, n_lon)
    mirror_nw = lax.rem(2 * n_lon - p, n_lon)
    ne_remote = jnp.logical_or(not_pole, mirror_ne != p)
    nw_remote = jnp.logical_or(not_pole, mirror_nw != p)
    ne_self = jnp.logical_and(at_pole, mirror_ne == p)
    nw_self = jnp.logical_and(at_pole, mirror_nw == p)

    barrier = pltpu.get_barrier_semaphore()

    def greet(lon, lat):
        pl.semaphore_signal(barrier, inc=1, device_id={"lon": lon, "lat": lat}, device_id_type=MESH)

    greet(east_dev, q)
    greet(west_dev, q)

    @pl.when(not_south)
    def _():
        for lon in (p, east_dev, west_dev):
            greet(lon, q - 1)

    @pl.when(not_pole)
    def _():
        for lon in (p, east_dev, west_dev):
            greet(lon, q + 1)

    @pl.when(at_pole)
    def _():
        greet(mirror, q)

    @pl.when(jnp.logical_and(at_pole, mirror_ne != p))
    def _():
        greet(mirror_ne, q)

    @pl.when(jnp.logical_and(at_pole, mirror_nw != p))
    def _():
        greet(mirror_nw, q)

    parity = lax.rem(q, 2)
    partner = q + 1 - 2 * parity
    n_half = n_lon * n_lat // 2
    me_half = (q // 2) * n_lon + p

    def half_peer(r):
        other = lax.rem(me_half + r, n_half)
        return lax.rem(other, n_lon), 2 * (other // n_lon) + parity

    def greet_half(r, carry):
        greet(*half_peer(r))
        return carry

    lax.fori_loop(1, n_half, greet_half, 0)
    greet(p, partner)

    for load in loads:
        load.wait()
    sub = iota((NI, NJ), 0)
    lane = iota((NI, NJ), 1)
    depth = (num_ref[...] * sea_ref[...]).astype(F32)
    height = jnp.zeros((NI, NJ), F32)
    for k in range(K):
        height = height + jnp.where(depth > k + 0.5, thick_ref[k], 0.0)
    early[parity, me_half, 0] = height
    early[parity, me_half, 1] = sea_ref[...].astype(F32) * eta_ref[...]
    early[parity, me_half, 2] = drive_ref[...]

    fields = (t_ref, s_ref, u_ref, v_ref)
    for pk, base, d1, d2 in ((epk, ebase, NI - 1, NI - 2), (wpk, wbase, 0, 1)):
        for c in range(NC):
            levels = slice(c * KC, (c + 1) * KC)
            for f, (ref, d) in enumerate(((t_ref, d1), (s_ref, d1), (u_ref, d1), (v_ref, d1), (u_ref, d2), (v_ref, d2))):
                pk[c, f * KC:(f + 1) * KC, :] = ref[levels, d, :]
        base[...] = jnp.where(sub == 0, depth[d1:d1 + 1, :], depth[d2:d2 + 1, :])

    n0 = jnp.zeros((NI, NJ), F32)
    s0 = jnp.zeros((NI, NJ), F32)
    n1 = jnp.zeros((NI, NJ), F32)
    s1 = jnp.zeros((NI, NJ), F32)

    def put(acc, x, source, target):
        moved = pltpu.roll(x, (target - source) % NJ, 1) if source != target else x
        return jnp.where(lane == target, moved, acc)

    for f, ref in enumerate(fields):
        for k in range(K):
            x = ref[k]
            target = f * K + k
            n0 = put(n0, x, NJ - 1, target)
            s0 = put(s0, x, 0, target)
            if f >= 2:
                n1 = put(n1, x, NJ - 2, target)
                s1 = put(s1, x, 1, target)
    n1 = put(put(n1, depth, NJ - 1, 0), depth, NJ - 2, 1)
    s1 = put(put(s1, depth, 0, 0), depth, 1, 1)
    npk[0] = n0
    npk[1] = n1
    spk[0] = s0
    spk[1] = s1

    peers = (3 + n_half + 2 * not_pole.astype(jnp.int32) + 3 * not_south.astype(jnp.int32)
             + at_pole.astype(jnp.int32) * ((mirror_ne != p).astype(jnp.int32) + (mirror_nw != p).astype(jnp.int32)))
    pl.semaphore_wait(barrier, peers)

    def copy(src, dst, lon, lat, out, into):
        return pltpu.make_async_remote_copy(
            src_ref=src, dst_ref=dst, send_sem=out, recv_sem=into,
            device_id={"lon": lon, "lat": lat}, device_id_type=MESH)

    def edge(src, slot, lon, lat, out):
        return copy(src, slots.at[slot], lon, lat, send_sem.at[out], recv_sem.at[slot])

    def side_east(c):
        return copy(epk.at[c], slot_w.at[c], east_dev, q, side_send.at[0, c], side_recv.at[0, c])

    def side_west(c):
        return copy(wpk.at[c], slot_e.at[c], west_dev, q, side_send.at[1, c], side_recv.at[1, c])

    base_east = copy(ebase, base_w, east_dev, q, send_sem.at[SEM_E], recv_sem.at[SEM_W])
    base_west = copy(wbase, base_e, west_dev, q, send_sem.at[SEM_W], recv_sem.at[SEM_E])
    base_east.start()
    base_west.start()
    side_east(0).start()
    side_west(0).start()

    @pl.when(not_south)
    def _():
        edge(spk, SLOT_N, p, q - 1, SLOT_S).start()
        edge(spk, SLOT_NW, east_dev, q - 1, SLOT_SE).start()
        edge(spk, SLOT_NE, west_dev, q - 1, SLOT_SW).start()

    @pl.when(not_pole)
    def _():
        edge(npk, SLOT_S, p, q + 1, SLOT_N).start()
        edge(npk, SLOT_SW, east_dev, q + 1, SLOT_NE).start()
        edge(npk, SLOT_SE, west_dev, q + 1, SLOT_NW).start()

    @pl.when(at_pole)
    def _():
        edge(npk, SLOT_N, mirror, q, SLOT_N).start()

    @pl.when(jnp.logical_and(at_pole, mirror_ne != p))
    def _():
        edge(npk, SLOT_NE, mirror_ne, q, SLOT_NE).start()

    @pl.when(jnp.logical_and(at_pole, mirror_nw != p))
    def _():
        edge(npk, SLOT_NW, mirror_nw, q, SLOT_NW).start()

    def cast(buf, which):
        def send(r, carry):
            lon, lat = half_peer(r)
            mine = buf.at[parity, me_half]
            pltpu.make_async_remote_copy(
                src_ref=mine, dst_ref=mine, send_sem=cast_send.at[which], recv_sem=cast_recv.at[which],
                device_id={"lon": lon, "lat": lat}, device_id_type=MESH).start()
            return carry

        lax.fori_loop(1, n_half, send, 0)

    def cast_wait(buf, sem):
        rest = buf.at[parity, pl.ds(0, n_half - 1)]
        pltpu.make_async_copy(rest, rest, sem).wait()

    def hand_over(buf, which):
        return pltpu.make_async_remote_copy(
            src_ref=buf.at[parity], dst_ref=buf.at[parity], send_sem=cast_send.at[which],
            recv_sem=cast_recv.at[which], device_id={"lon": p, "lat": partner}, device_id_type=MESH)

    for c in range(1, NC):
        side_east(c).start()
        side_west(c).start()

    edge(npk, SLOT_N, p, q, SLOT_N).wait_recv()

    @pl.when(ne_remote)
    def _():
        edge(npk, SLOT_NE, p, q, SLOT_NE).wait_recv()

    @pl.when(nw_remote)
    def _():
        edge(npk, SLOT_NW, p, q, SLOT_NW).wait_recv()

    @pl.when(not_south)
    def _():
        for slot in (SLOT_S, SLOT_SE, SLOT_SW):
            edge(spk, slot, p, q, slot).wait_recv()

    sign = jnp.where(lane >= 2 * K, -1.0, 1.0).astype(F32)

    def northern(slot, own):
        out = []
        for i in range(2):
            x = slots[slot, i]
            if own is not None:
                x = jnp.where(own, npk[i], x)
            out.append(jnp.where(at_pole, flip_rows(x) * sign, x))
        return out

    def southern(slot):
        return [jnp.where(not_south, slots[slot, i], 0.0) for i in range(2)]

    pn0, pn1 = northern(SLOT_N, None)
    pne0, pne1 = northern(SLOT_NE, ne_self)
    pnw0, pnw1 = northern(SLOT_NW, nw_self)
    ps0, ps1 = southern(SLOT_S)
    pse0, pse1 = southern(SLOT_SE)
    psw0, psw1 = southern(SLOT_SW)

    def shift_e(x, row):
        return jnp.where(sub == NI - 1, row, pltpu.roll(x, NI - 1, 0))

    def shift_w(x, row):
        return jnp.where(sub == 0, row, pltpu.roll(x, 1, 0))

    level_l = (lane - K * (lane // K)).astype(F32) + 0.5

    def wet_l(d):
        return jnp.where(level_l < d, 1.0, 0.0)

    def spread(x, i):
        return jnp.broadcast_to(x[:, i:i + 1], (NI, NJ))

    def packed_lap(c0, c1, e0, e1, w0, w1, own, own_depth):
        d = spread(c1, 0)
        de = shift_e(d, jnp.broadcast_to(e1[0:1, 0:1], (NI, NJ)))
        dw = shift_w(d, jnp.broadcast_to(w1[NI - 1:NI, 0:1], (NI, NJ)))
        xe = shift_e(c0, jnp.broadcast_to(e0[0:1, :], (NI, NJ)))
        xw = shift_w(c0, jnp.broadcast_to(w0[NI - 1:NI, :], (NI, NJ)))
        total = wet_l(de) * (xe - c0) + wet_l(dw) * (xw - c0)
        total = total + wet_l(spread(c1, 1)) * (c1 - c0) + wet_l(own_depth) * (own - c0)
        return wet_l(d) * total

    lap_n = packed_lap(pn0, pn1, pne0, pne1, pnw0, pnw1, n0, spread(depth, NJ - 1))
    lap_s = packed_lap(ps0, ps1, pse0, pse1, psw0, psw1, s0, spread(depth, 0))
    rim[4, 0:NI, :] = lap_n
    rim[5, 0:NI, :] = lap_s
    rim[4, NI:2 * NI, :] = pn0
    rim[5, NI:2 * NI, :] = ps0

    base_east.wait_recv()
    base_west.wait_recv()

    row_c = iota((KC, NJ), 0)
    lane_c = iota((KC, NJ), 1)

    def wide(row):
        return jnp.broadcast_to(row, (KC, NJ))

    rim[6, 0:NI, :] = pne0
    rim[6, NI:2 * NI, :] = pse0
    rim[7, 0:NI, :] = pnw0
    rim[7, NI:2 * NI, :] = psw0
    side_depths = []
    for base, d1, cn1, cs1 in ((base_e, NI - 1, pne1[0:1], pse1[0:1]), (base_w, 0, pnw1[NI - 1:], psw1[NI - 1:])):
        d = wide(base[0:1, :])
        dn = jnp.where(lane_c == NJ - 1, jnp.broadcast_to(cn1[:, 0:1], (KC, NJ)), pltpu.roll(d, NJ - 1, 1))
        ds = jnp.where(lane_c == 0, jnp.broadcast_to(cs1[:, 0:1], (KC, NJ)), pltpu.roll(d, 1, 1))
        side_depths.append((d, wide(base[1:2, :]), wide(depth[d1:d1 + 1, :]), dn, ds))

    def side_laps(c):
        level_c = (row_c + c * KC).astype(F32) + 0.5
        for side, (slot, pk, corner) in enumerate(((slot_e, epk, 0), (slot_w, wpk, NI - 1))):
            mid, far, own, mn, ms = [jnp.where(level_c < d, 1.0, 0.0) for d in side_depths[side]]
            cn0 = rim[6 + side, corner:corner + 1, :]
            cs0 = rim[6 + side, NI + corner:NI + corner + 1, :]
            for i in range(2):
                f = 2 + i
                x = slot[c, f * KC:(f + 1) * KC, :]
                pick = lane_c == row_c + (c * KC + f * K)
                cn = jnp.sum(jnp.where(pick, wide(cn0), 0.0), axis=1, keepdims=True)
                cs = jnp.sum(jnp.where(pick, wide(cs0), 0.0), axis=1, keepdims=True)
                xn = jnp.where(lane_c == NJ - 1, jnp.broadcast_to(cn, (KC, NJ)), pltpu.roll(x, NJ - 1, 1))
                xs = jnp.where(lane_c == 0, jnp.broadcast_to(cs, (KC, NJ)), pltpu.roll(x, 1, 1))
                total = far * (slot[c, (4 + i) * KC:(5 + i) * KC, :] - x)
                total = total + own * (pk[c, f * KC:(f + 1) * KC, :] - x) + mn * (xn - x) + ms * (xs - x)
                rim[2 * side + i, 0:KC, :] = mid * total

    def shift_n(x, packed, source):
        return jnp.where(lane == NJ - 1, pltpu.roll(packed, NJ - 1 - source, 1), pltpu.roll(x, NJ - 1, 1))

    def shift_s(x, packed, source):
        return jnp.where(lane == 0, pltpu.roll(packed, lax.rem(NJ - source, NJ), 1), pltpu.roll(x, 1, 1))

    depth_e = shift_e(depth, base_e[0:1, :])
    depth_w = shift_w(depth, base_w[0:1, :])
    depth_n = shift_n(depth, pn1, 0)
    depth_s = jnp.where(lane == 0, ps1, pltpu.roll(depth, 1, 1))
    both_e = jnp.minimum(depth, depth_e)
    both_w = jnp.minimum(depth, depth_w)
    both_n = jnp.minimum(depth, depth_n)
    both_s = jnp.minimum(depth, depth_s)
    lat_index = (q * NJ + lane).astype(F32)
    coriolis = CORIOLIS * (2.0 * (lat_index + 0.5) / (n_lat * NJ) - 1.0)

    zero = jnp.zeros((NI, NJ), F32)
    cast(early, 0)

    def around(c, inner, ref, f):
        k = c * KC + inner
        x = ref[k]
        row = f * KC + inner
        return (x, shift_e(x, slot_e[c, row:row + 1, :]), shift_w(x, slot_w[c, row:row + 1, :]),
                shift_n(x, rim[4, NI:2 * NI, :], f * K + k), shift_s(x, rim[5, NI:2 * NI, :], f * K + k))

    def tracers(c, i, carry):
        k = c * KC + i
        flux_t, flux_s = carry
        kf = lax.convert_element_type(k, F32) + 0.5
        h = thick_ref[k]
        nxt = jnp.minimum(k + 1, K - 1)
        h_next = thick_ref[nxt]
        hv = jnp.full((NI, NJ), h, F32)
        inv_space = 1.0 / (0.5 * (hv + h_next))
        inv_h = MIXING / hv

        def wet(d):
            return jnp.where(d > kf, 1.0, 0.0)

        mc = wet(depth)
        me, mw, mn, ms = wet(both_e), wet(both_w), wet(both_n), wet(both_s)
        below = jnp.where(jnp.logical_and(depth > kf + 1.0, k < K - 1), inv_space, 0.0)
        t = around(c, i, t_ref, 0)
        s = around(c, i, s_ref, 1)
        u0, ue, uw = around(c, i, u_ref, 2)[:3]
        v0, _, _, vn, vs = around(c, i, v_ref, 3)
        ae = 0.25 * me * (u0 + ue)
        aw = 0.25 * mw * (u0 + uw)
        an = 0.25 * mn * (v0 + vn)
        as_ = 0.25 * ms * (v0 + vs)
        ge, gw, gn, gs = DIFFUSION * me, DIFFUSION * mw, DIFFUSION * mn, DIFFUSION * ms

        def tracer(x, ref, flux_above):
            c, e, w, n, so = x
            total = aw * (w + c) - gw * (c - w) - ae * (c + e) + ge * (e - c)
            total = total + as_ * (so + c) - gs * (c - so) - an * (c + n) + gn * (n - c)
            flux = below * (ref[nxt] - c)
            return mc * (c + total + inv_h * (flux - flux_above)), flux

        new_t, flux_t = tracer(t, t_ref, flux_t)
        new_s, flux_s = tracer(s, s_ref, flux_s)
        ot_ref[k] = new_t
        os_ref[k] = new_s
        return flux_t, flux_s

    def level(c, i, carry):
        k = c * KC + i
        inner = i
        pc, pe, pw, pn_, ps_, tu, tv = carry
        kf = lax.convert_element_type(k, F32) + 0.5
        h = thick_ref[k]

        def wet(d):
            return jnp.where(d > kf, 1.0, 0.0)

        mc = wet(depth)
        me, mw, mn, ms = wet(both_e), wet(both_w), wet(both_n), wet(both_s)
        lapn = rim[4, 0:NI, :]
        laps = rim[5, 0:NI, :]
        t = around(c, i, t_ref, 0)
        s = around(c, i, s_ref, 1)
        u = around(c, i, u_ref, 2)
        v = around(c, i, v_ref, 3)
        pressures = []
        for i, (acc, d) in enumerate(((pc, depth), (pe, depth_e), (pw, depth_w), (pn_, depth_n), (ps_, depth_s))):
            density = CONTRACTION * s[i] - EXPANSION * t[i]
            pressures.append(acc + jnp.where(d > kf, density * h, 0.0))
        pc, pe, pw, pn_, ps_ = pressures
        grad_x = 0.5 * (me * (pe - pc) + mw * (pc - pw))
        grad_y = 0.5 * (mn * (pn_ - pc) + ms * (pc - ps_))

        def biharmonic(x, i):
            c, e, w, n, so = x
            lap = me * (e - c) + mw * (w - c) + mn * (n - c) + ms * (so - c)
            le = shift_e(lap, rim[i, inner:inner + 1, :])
            lw = shift_w(lap, rim[2 + i, inner:inner + 1, :])
            source = (2 + i) * K + k
            ln = shift_n(lap, lapn, source)
            ls = shift_s(lap, laps, source)
            return me * (le - lap) + mw * (lw - lap) + mn * (ln - lap) + ms * (ls - lap)

        u_star = mc * (u[0] + coriolis * v[0] - PRESSURE_SCALE * grad_x - FRICTION * biharmonic(u, 0))
        v_star = mc * (v[0] - coriolis * u[0] - PRESSURE_SCALE * grad_y - FRICTION * biharmonic(v, 1))
        ou_ref[k] = u_star
        ov_ref[k] = v_star
        return (pc, pe, pw, pn_, ps_, tu + h * u_star, tv + h * v_star)

    def chunk(c, carry):
        side_east(c).wait_recv()
        side_west(c).wait_recv()
        side_laps(c)
        for i in range(KC):
            carry = level(c, i, carry)
        return carry

    carry = lax.fori_loop(0, NC, chunk, (zero,) * 7)
    late[parity, me_half, 0] = carry[5]
    late[parity, me_half, 1] = carry[6]
    cast(late, 1)

    def tracer_chunk(c, carry):
        for i in range(KC):
            carry = tracers(c, i, carry)
        return carry

    lax.fori_loop(0, NC, tracer_chunk, (zero,) * 2)

    cast_wait(early, cast_recv.at[0])
    early_over = hand_over(early, 2)
    early_over.start()
    early_over.wait_recv()

    def loader(buf, count):
        flat = buf.reshape(2 * n_half * count * NI, NJ)

        def load(f):
            return [[flat[pl.ds((((b % 2) * n_half + (b // 2) * n_lon) * count + f) * NI + s, n_lon,
                                stride=count * NI), :] for s in range(NI)] for b in range(n_lat)]

        return load

    def late_loader():
        cast_wait(late, cast_recv.at[1])
        late_over = hand_over(late, 3)
        late_over.start()
        late_over.wait_recv()
        return loader(late, LATE)

    x, slope_x, slope_y, rms = surface_solve(loader(early, EARLY), late_loader, n_lon, n_lat, K, NI, NJ,
                                             n_lon * NI * n_lat * NJ)
    for i, field in enumerate((x, slope_x, slope_y)):
        for b in range(n_lat):
            for s in range(NI):
                held[i, b, pl.ds(s, n_lon, stride=NI), :] = field[b][s]
    block = pl.ds(pl.multiple_of(p * NI, NI), NI)
    ox_ref[0] = held[0, q, block, :]
    ox_ref[1] = GRAVITY * held[1, q, block, :]
    ox_ref[2] = GRAVITY * held[2, q, block, :]
    ox_ref[3] = jnp.broadcast_to(rms, (NI, NJ))
    ox_ref[4] = depth

    cast_wait(early, cast_send.at[0])
    cast_wait(late, cast_send.at[1])
    early_over.wait_send()
    hand_over(late, 3).wait_send()

    base_east.wait_send()
    base_west.wait_send()
    for c in range(NC):
        side_east(c).wait_send()
        side_west(c).wait_send()

    @pl.when(not_south)
    def _():
        for out in (SLOT_S, SLOT_SE, SLOT_SW):
            edge(spk, SLOT_N, p, q, out).wait_send()

    edge(npk, SLOT_N, p, q, SLOT_N).wait_send()

    @pl.when(ne_remote)
    def _():
        edge(npk, SLOT_NE, p, q, SLOT_NE).wait_send()

    @pl.when(nw_remote)
    def _():
        edge(npk, SLOT_NW, p, q, SLOT_NW).wait_send()


def surface_solve(load, load_late, n_lon, n_lat, K, NI, NJ, cells):
    tiles = range(n_lat)
    lines = range(NI)
    lane = iota((n_lon, NJ), 1)

    def every(fn, *arrays):
        return [[fn(*(a[b][s] for a in arrays)) for s in lines] for b in tiles]

    def east(x):
        return [x[b][1:] + [pltpu.roll(x[b][0], n_lon - 1, 0)] for b in tiles]

    def west(x):
        return [[pltpu.roll(x[b][NI - 1], 1, 0)] + x[b][:-1] for b in tiles]

    def north(x, sign):
        out = []
        for b in tiles:
            row = []
            for s in lines:
                if b + 1 < n_lat:
                    beyond = pltpu.roll(x[b + 1][s], NJ - 1, 1)
                else:
                    beyond = flip_rows(x[b][NI - 1 - s])
                    beyond = -beyond if sign < 0 else beyond
                row.append(jnp.where(lane == NJ - 1, beyond, pltpu.roll(x[b][s], NJ - 1, 1)))
            out.append(row)
        return out

    def south(x):
        out = []
        for b in tiles:
            row = []
            for s in lines:
                beyond = pltpu.roll(x[b - 1][s], 1, 1) if b > 0 else 0.0
                row.append(jnp.where(lane == 0, beyond, pltpu.roll(x[b][s], 1, 1)))
            out.append(row)
        return out

    height = load(0)
    scale = lambda a, c: jnp.minimum(a, c) * (1.0 / K)
    w_e = every(scale, height, east(height))
    w_w = every(scale, height, west(height))
    w_n = every(scale, height, north(height, 1))
    w_s = every(scale, height, south(height))
    diag = every(lambda a, b, c, d: STORAGE + a + b + c + d, w_e, w_w, w_n, w_s)

    def apply(x):
        return every(
            lambda dg, c, we, e, ww, w, wn, n, ws, s: dg * c - (we * e + ww * w + wn * n + ws * s),
            diag, x, w_e, east(x), w_w, west(x), w_n, north(x, 1), w_s, south(x))

    factors = [[None] * NI for _ in tiles]
    pivots = [[None] * NI for _ in tiles]
    for b in tiles:
        for s in lines:
            pivot = diag[b][s]
            if s > 0:
                pivot = pivot + w_w[b][s] * factors[b][s - 1]
            pivots[b][s] = 1.0 / pivot
            factors[b][s] = -w_e[b][s] * pivots[b][s]

    def precondition(r):
        out = []
        for b in tiles:
            part = []
            for s in lines:
                value = r[b][s]
                if s > 0:
                    value = value + w_w[b][s] * part[s - 1]
                part.append(value * pivots[b][s])
            for s in range(NI - 2, -1, -1):
                part[s] = part[s] - factors[b][s] * part[s + 1]
            out.append(part)
        return out

    x = load(1)
    drive = load(2)
    start = every(lambda h, d, a: jnp.where(h > 0.0, d, 0.0) - a, height, drive, apply(x))
    load = load_late()
    t_u = load(0)
    t_v = load(1)
    residual = every(
        lambda h, d, e, w, n, s: d - jnp.where(h > 0.0, 0.5 * DIVERGENCE * ((e - w) + (n - s)), 0.0),
        height, start, east(t_u), west(t_u), north(t_v, -1), south(t_v))
    mid = 0.5 * (SPECTRUM_HIGH + SPECTRUM_LOW)
    half = 0.5 * (SPECTRUM_HIGH - SPECTRUM_LOW)
    ratio = mid / half
    direction = every(lambda a: a / mid, precondition(residual))
    rho = 1.0 / ratio
    for step in range(ITERS):
        x = every(lambda a, b: a + b, x, direction)
        residual = every(lambda a, b: a - b, residual, apply(direction))
        if step + 1 < ITERS:
            rho_next = 1.0 / (2.0 * ratio - rho)
            keep, gain = rho_next * rho, 2.0 * rho_next / half
            direction = every(lambda d, z: keep * d + gain * z, direction, precondition(residual))
            rho = rho_next
    squares = every(lambda a: a * a, residual)
    total = functools.reduce(lambda a, b: a + b, [squares[b][s] for b in tiles for s in lines])
    total = jnp.sum(jnp.sum(total, axis=1, keepdims=True), axis=0, keepdims=True)
    rms = jnp.sqrt(total / cells + EPSILON)
    slope_x = every(lambda e, w: 0.5 * (e - w), east(x), west(x))
    slope_y = every(lambda n, s: 0.5 * (n - s), north(x, 1), south(x))
    return x, slope_x, slope_y, rms


def finish_kernel(KC, t_ref, s_ref, u_ref, v_ref, x_ref, ot_ref, os_ref, ou_ref, ov_ref, ox_ref, orms_ref,
                  bufs, plain_sem, chunk_sem):
    plain = [pltpu.make_async_copy(src, dst, plain_sem.at[i])
             for i, (src, dst) in enumerate(((t_ref, ot_ref), (s_ref, os_ref), (x_ref.at[0], ox_ref)))]
    for copy in plain:
        copy.start()
    depth = x_ref[4]
    K = t_ref.shape[0]
    chunks = []
    for c in range(K // KC):
        levels = pl.ds(c * KC, KC)
        for f, (src, dst) in enumerate(((u_ref, ou_ref), (v_ref, ov_ref))):
            slope = x_ref[1 + f]
            for k in range(c * KC, (c + 1) * KC):
                bufs[f, k] = jnp.where(depth > k + 0.5, src[k] - slope, 0.0)
            copy = pltpu.make_async_copy(bufs.at[f, levels], dst.at[levels], chunk_sem.at[f, c])
            copy.start()
            chunks.append(copy)
    orms_ref[0] = jnp.max(x_ref[3])
    for copy in plain + chunks:
        copy.wait()


def per_device(n_lon, n_lat, temp, salt, u, v, num, sea, thick, eta, drive):
    K, NI, NJ = temp.shape
    KC = 8 if K % 8 == 0 else K
    NC = K // KC
    n_half = n_lon * n_lat // 2
    vmem = pl.BlockSpec(memory_space=pltpu.VMEM)
    smem = pl.BlockSpec(memory_space=pltpu.SMEM)
    anywhere = pl.BlockSpec(memory_space=pltpu.HBM)
    big = jax.ShapeDtypeStruct((K, NI, NJ), F32)
    kept = pltpu.VMEM((K, NI, NJ), F32)
    flat = jax.ShapeDtypeStruct((NI, NJ), F32)
    one = jax.ShapeDtypeStruct((1,), F32)
    args = (temp, salt, u, v, num, sea, thick, eta, drive)
    sides = pltpu.VMEM((NC, 6 * KC, NJ), F32)
    tile = pltpu.VMEM((NI, NJ), F32)
    parts = pl.pallas_call(
        functools.partial(step_kernel, n_lon, n_lat, KC),
        out_shape=(kept, kept, kept, kept, pltpu.VMEM((5, NI, NJ), F32)),
        in_specs=[anywhere] * 9,
        out_specs=(vmem,) * 5,
        scratch_shapes=[(pltpu.SMEM if a.ndim == 1 else pltpu.VMEM)(a.shape, a.dtype) for a in args] + [
            sides, sides, tile, tile,
            pltpu.VMEM((2, NI, NJ), F32), pltpu.VMEM((2, NI, NJ), F32),
            sides, sides, tile, tile,
            pltpu.VMEM((6, 2, NI, NJ), F32), pltpu.VMEM((8, max(KC, 2 * NI), NJ), F32),
            pltpu.VMEM((2, n_half, EARLY, NI, NJ), F32), pltpu.VMEM((2, n_half, LATE, NI, NJ), F32),
            pltpu.VMEM((3, n_lat, n_lon * NI, NJ), F32),
            pltpu.SemaphoreType.DMA((9,)),
            pltpu.SemaphoreType.DMA((8,)), pltpu.SemaphoreType.DMA((8,)),
            pltpu.SemaphoreType.DMA((2, NC)), pltpu.SemaphoreType.DMA((2, NC)),
            pltpu.SemaphoreType.DMA((4,)), pltpu.SemaphoreType.DMA((4,)),
        ],
        compiler_params=pltpu.CompilerParams(
            collective_id=0, has_side_effects=True),
        name="step",
    )(*args)
    outs = pl.pallas_call(
        functools.partial(finish_kernel, KC),
        out_shape=(big, big, big, big, flat, one),
        in_specs=[vmem] * 5,
        out_specs=(anywhere,) * 5 + (smem,),
        scratch_shapes=[pltpu.VMEM((2, K, NI, NJ), F32), pltpu.SemaphoreType.DMA((3,)),
                        pltpu.SemaphoreType.DMA((2, NC))],
        name="finish",
    )(*[pltpu.with_memory_space_constraint(part, pltpu.VMEM) for part in parts])
    return outs[:5] + (outs[5].reshape(()),)


def solution(mesh):
    n_lon, n_lat = mesh.shape["lon"], mesh.shape["lat"]
    spec3 = P(None, "lon", "lat")
    spec2 = P("lon", "lat")
    return jax.shard_map(
        functools.partial(per_device, n_lon, n_lat),
        mesh=mesh,
        in_specs=(spec3, spec3, spec3, spec3, spec2, spec2, P(), spec2, spec2),
        out_specs=(spec3, spec3, spec3, spec3, spec2, P()),
        check_vma=False,
    )
```

profile of v0, /device:TPU:0, one launch (start us, length us, event | category | flops | bytes accessed | tf_op | source)
XLA Modules:
  0.0 25.0 jit_solution(6317786379675617291)
XLA Ops:
  0.6 22.9 %step.1 = (f32[32,8,128]{2,1,0:T(8,128)S(1)}, f32[32,8,128]{2,1,0:T(8,128)S(1)}, f32[32,8,128]{2,1,0:T(8,128)S(1)}, f32[32,8,128]{2,1,0:T(8,128)S(1)}, f32[5,8,128]{2,1,0:T(8,128)S(1)}) custom-call(f32[32,8,128]{2,1,0:T(8,128)} %refs_0_.1, f32[32,8,128]{2,1,0:T(8,128)} %refs_1_.1, f32[32,8,128]{2,1,0:T(8,128)} %refs_2_.1, f32[32,8,128]{2,1,0:T(8,128)} %refs_3_.1, ...), custom_call_target="tpu_custom_call" | custom-call | tf_op jit(solution)/shard_map/step/pallas_call | solution.py:679
  23.6 1.4 %finish.1 = (f32[32,8,128]{2,1,0:T(8,128)}, f32[32,8,128]{2,1,0:T(8,128)}, f32[32,8,128]{2,1,0:T(8,128)}, f32[32,8,128]{2,1,0:T(8,128)}, f32[8,128]{1,0:T(8,128)}, /*index=5*/f32[1]{0:T(128)}) custom-call(f32[32,8,128]{2,1,0:T(8,128)S(1)} %get-tuple-element.17.t_ref, f32[32,8,128]{2,1,0:T(8,128)S(1)} %get-tuple-element.18.s_ref, ...), custom_call_target="tpu_custom_call" | custom-call | tf_op jit(solution)/shard_map/finish/pallas_call | solution.py:700
where the time goes:
time: 25.1 us; the launch traced here: 25 us
  Pallas kernels  24.3 us (97%)
  between operations  0.64 us (3%)
    pallas_call x1, Pallas kernels, per_device(): pl.pallas_call(functools.partial(step_kernel, n_lon, n_lat, KC), out_shap...  22.9 us
    pallas_call x1, Pallas kernels, per_device(): pl.pallas_call(functools.partial(finish_kernel, KC), out_shape=(big, big,...  1.4 us

commit v1 on v0

v1 whole, which is shorter than its diff:
```python
import functools

import jax
import jax.numpy as jnp
from jax import lax
from jax.experimental import pallas as pl
from jax.experimental.pallas import tpu as pltpu
from jax.sharding import PartitionSpec as P

ITERS = 4
DIFFUSION = 0.15
MIXING = 0.1
EXPANSION = 0.2
CONTRACTION = 0.15
PRESSURE_SCALE = 0.02
CORIOLIS = 0.5
FRICTION = 0.01
DIVERGENCE = 0.3
STORAGE = 0.1
SPECTRUM_LOW = 0.1
SPECTRUM_HIGH = 1.9
GRAVITY = 0.3
EPSILON = 1e-06

MESH = pl.DeviceIdType.MESH
F32 = jnp.float32
SLOT_N, SLOT_NE, SLOT_NW, SLOT_S, SLOT_SE, SLOT_SW = range(6)
EARLY = 3
LATE = 2
TILES = EARLY + LATE + 1


def iota(shape, axis):
    return lax.broadcasted_iota(jnp.int32, shape, axis)


def flip_rows(x):
    n = x.shape[0]
    row = iota(x.shape, 0)
    bit = n // 2
    while bit:
        up = pltpu.roll(x, bit, 0)
        down = pltpu.roll(x, n - bit, 0)
        x = up if 2 * bit == n else jnp.where((row & bit) != 0, up, down)
        bit //= 2
    return x


def flip_lanes(x):
    n = x.shape[1]
    lane = iota(x.shape, 1)
    bit = n // 2
    while bit:
        up = pltpu.roll(x, bit, 1)
        x = up if 2 * bit == n else jnp.where((lane & bit) != 0, up, pltpu.roll(x, n - bit, 1))
        bit //= 2
    return x


def step_kernel(n_lon, n_lat, KC, *refs):
    sources, refs = refs[:9], refs[9:]
    (kept, ox_ref), refs = refs[:2], refs[2:]
    (fields, ints, floats, thick_ref, pack_out, pack_in, edges, slots, rim, side_lap, laps, pressure, tiles, strips,
     rims, sums, held, load_sem, send_sem, chunk_sem, edge_sem, cast_send, cast_recv) = refs
    _, K, NI, NJ = fields.shape
    NC = K // KC
    SIDE = 3 * KC
    BASE = NC * SIDE
    REST = BASE + NI
    t_ref, s_ref, u_ref, v_ref = (fields.at[f] for f in range(4))
    ot_ref, os_ref, ou_ref, ov_ref = (kept.at[f] for f in range(4))
    num_ref, sea_ref, eta_ref, drive_ref = ints.at[0], ints.at[1], floats.at[0], floats.at[1]
    p = lax.axis_index("lon")
    q = lax.axis_index("lat")
    east_dev = lax.rem(p + 1, n_lon)
    west_dev = lax.rem(p + n_lon - 1, n_lon)
    at_pole = q == n_lat - 1
    not_pole = q < n_lat - 1
    not_south = q > 0
    mirror = n_lon - 1 - p
    mirror_ne = lax.rem(2 * n_lon - 2 - p, n_lon)
    mirror_nw = lax.rem(2 * n_lon - p, n_lon)
    ne_remote = jnp.logical_or(not_pole, mirror_ne != p)
    nw_remote = jnp.logical_or(not_pole, mirror_nw != p)
    both_remote = jnp.logical_and(ne_remote, nw_remote)
    one_remote = jnp.logical_not(both_remote)
    ne_self = jnp.logical_and(at_pole, mirror_ne == p)
    nw_self = jnp.logical_and(at_pole, mirror_nw == p)

    barrier = pltpu.get_barrier_semaphore()

    def greet(lon, lat):
        pl.semaphore_signal(barrier, inc=1, device_id={"lon": lon, "lat": lat}, device_id_type=MESH)

    greet(east_dev, q)
    if n_lon > 2:
        greet(west_dev, q)

    def around_lon(first, last, fn):
        def visit(r, carry):
            fn(lax.rem(p + r, n_lon))
            return carry

        if last - first <= 8:
            for r in range(first, last):
                visit(r, 0)
        else:
            lax.fori_loop(first, last, visit, 0)

    @pl.when(at_pole)
    def _():
        around_lon(2, n_lon - 1, lambda lon: greet(lon, q))

    @pl.when(not_south)
    def _():
        around_lon(0, n_lon, lambda lon: greet(lon, q - 1))

    @pl.when(not_pole)
    def _():
        around_lon(0, n_lon, lambda lon: greet(lon, q + 1))

    def load(i, dst, sem):
        pltpu.make_async_copy(sources[i], dst, load_sem.at[sem]).start()

    load(4, num_ref, 1)
    load(5, sea_ref, 1)
    load(7, eta_ref, 1)
    load(8, drive_ref, 1)
    for f in (2, 3, 0, 1):
        load(f, fields.at[f], 0)
    thick_load = pltpu.make_async_copy(sources[6], thick_ref, load_sem.at[2])
    thick_load.start()

    @pl.when(not_pole)
    def _():
        around_lon(2, n_lon - 1, lambda lon: greet(lon, q))

    for lat in range(n_lat):
        @pl.when(jnp.logical_or(q - lat > 1, lat - q > 1))
        def _():
            greet(p, lat)

    def drain(ref, sem):
        pltpu.make_async_copy(ref, ref, sem).wait()

    thick_load.wait()
    drain(fields.at[0, 0:4], load_sem.at[1])
    drain(fields, load_sem.at[0])
    sub = iota((NI, NJ), 0)
    lane = iota((NI, NJ), 1)
    depth = (num_ref[...] * sea_ref[...]).astype(F32)

    row_c = iota((KC, NJ), 0)
    lane_c = iota((KC, NJ), 1)
    thick_c = []
    for c in range(NC):
        h = jnp.zeros((KC, NJ), F32)
        for i in range(KC):
            h = jnp.where(row_c == i, thick_ref[c * KC + i], h)
        thick_c.append(h)

    def wide(row):
        return jnp.broadcast_to(row, (KC, NJ))

    for side, (d1, d2) in enumerate(((NI - 1, NI - 2), (0, 1))):
        own_depth = wide(depth[d1:d1 + 1, :])
        carried = jnp.zeros((KC, NJ), F32)
        for c in range(NC):
            levels = slice(c * KC, (c + 1) * KC)
            row = c * SIDE
            pack_out[side, row:row + KC, :] = u_ref[levels, d1, :]
            pack_out[side, row + KC:row + 2 * KC, :] = v_ref[levels, d1, :]
            t_col, s_col = t_ref[levels, d1, :], s_ref[levels, d1, :]
            wet = own_depth > row_c.astype(F32) + (c * KC + 0.5)
            x = jnp.where(wet, (CONTRACTION * s_col - EXPANSION * t_col) * thick_c[c], 0.0)
            step = 1
            while step < KC:
                x = x + jnp.where(row_c >= step, pltpu.roll(x, step, 0), 0.0)
                step *= 2
            x = x + carried
            pack_out[side, row + 2 * KC:row + 3 * KC, :] = x
            carried = wide(x[KC - 1:KC, :])
            for f, (ref, d) in enumerate(((u_ref, d2), (v_ref, d2))):
                row = REST + (2 + f) * K + c * KC
                pack_out[side, row:row + KC, :] = ref[levels, d, :]
            for f, x in enumerate((t_col, s_col)):
                row = REST + f * K + c * KC
                pack_out[side, row:row + KC, :] = x
        pack_out[side, BASE:REST, :] = jnp.where(sub == 0, depth[d1:d1 + 1, :], depth[d2:d2 + 1, :])

    zero = jnp.zeros((NI, NJ), F32)

    def put(acc, x, source, target):
        moved = pltpu.roll(x, (target - source) % NJ, 1) if source != target else x
        return jnp.where(lane == target, moved, acc)

    n0 = s0 = n1 = s1 = zero
    for f, ref in enumerate((t_ref, s_ref, u_ref, v_ref)):
        for k in range(K):
            x = ref[k]
            target = f * K + k
            n0 = put(n0, x, NJ - 1, target)
            s0 = put(s0, x, 0, target)
            if f >= 2:
                n1 = put(n1, x, NJ - 2, target)
                s1 = put(s1, x, 1, target)
    n1 = put(put(n1, depth, NJ - 1, 0), depth, NJ - 2, 1)
    s1 = put(put(s1, depth, 0, 0), depth, 1, 1)
    npk, spk = edges.at[0], edges.at[1]
    npk[0] = n0
    npk[1] = n1
    spk[0] = s0
    spk[1] = s1

    peers = n_lon + n_lat - 2 + (n_lon - 1) * (not_south.astype(jnp.int32) + not_pole.astype(jnp.int32))
    pl.semaphore_wait(barrier, peers)

    def copy(src, dst, lon, lat, out, into):
        return pltpu.make_async_remote_copy(
            src_ref=src, dst_ref=dst, send_sem=out, recv_sem=into,
            device_id={"lon": lon, "lat": lat}, device_id_type=MESH)

    def edge(src, slot, lon, lat, out, row=None):
        dst = slots.at[slot]
        if slot in (SLOT_NE, SLOT_SE, SLOT_NW, SLOT_SW):
            if row is None:
                row = 0 if slot in (SLOT_NE, SLOT_SE) else NI - 1
            src, dst = src.at[:, row:row + 1, :], dst.at[:, row:row + 1, :]
        into = 0 if slot in (SLOT_N, SLOT_NE, SLOT_NW) else 1
        copy(src, dst, lon, lat, send_sem.at[out], edge_sem.at[into]).start()

    @pl.when(at_pole)
    def _():
        edge(npk, SLOT_N, mirror, q, 2)

    @pl.when(jnp.logical_and(at_pole, mirror_ne != p))
    def _():
        edge(npk, SLOT_NE, mirror_ne, q, 2, NI - 1)

    @pl.when(jnp.logical_and(at_pole, mirror_nw != p))
    def _():
        edge(npk, SLOT_NW, mirror_nw, q, 2, 0)

    @pl.when(not_south)
    def _():
        edge(spk, SLOT_NW, east_dev, q - 1, 1)
        edge(spk, SLOT_NE, west_dev, q - 1, 1)
        edge(spk, SLOT_N, p, q - 1, 1)

    @pl.when(not_pole)
    def _():
        edge(npk, SLOT_SW, east_dev, q + 1, 2)
        edge(npk, SLOT_SE, west_dev, q + 1, 2)
        edge(npk, SLOT_S, p, q + 1, 2)

    def sides(first, rows, sem):
        rows = pl.ds(first, rows)
        copy(pack_out.at[0, rows], pack_in.at[1, rows], east_dev, q, send_sem.at[0], chunk_sem.at[sem]).start()
        copy(pack_out.at[1, rows], pack_in.at[0, rows], west_dev, q, send_sem.at[0], chunk_sem.at[sem]).start()

    sides(BASE, NI, NC)
    for c in range(NC):
        sides(c * SIDE, SIDE, c)

    height = zero
    for k in range(K):
        height = height + jnp.where(depth > k + 0.5, thick_ref[k], 0.0)
    width = NJ // NI
    in_block = lane // width == sub
    parts = ((0, EARLY, EARLY * NI), (EARLY, LATE + 1, LATE * NI + 4))

    def pack_strips(which, sign, *arrays):
        first, count, _ = parts[which]
        south = zero
        north = zero
        for i, x in enumerate(arrays):
            for start in (0, width):
                moved = pltpu.roll(x, start, 1, stride=width, stride_axis=0)
                row = jnp.sum(jnp.where(in_block, moved, 0.0), axis=0, keepdims=True)
                row = jnp.broadcast_to(row, (NI, NJ))
                if start:
                    north = jnp.where(sub == i, row, north)
                else:
                    south = jnp.where(sub == i, row, south)
        north = jnp.where(at_pole, sign * flip_lanes(north), north)
        rows = slice(first, first + count)
        strips[0, rows] = south[:count]
        strips[1, rows] = north[:count]

        @pl.when(at_pole)
        def _():
            rims[0, mirror, rows] = north[:count]

    def cast(which):
        first, _, size = parts[which]
        mine = tiles.at[p, pl.ds(first * NI, size)]
        around_lon(1, n_lon, lambda lon: copy(mine, mine, lon, q, cast_send.at[0], cast_recv.at[which, 0]).start())

    def cast_strips(which):
        first, count, _ = parts[which]
        rows = pl.ds(first, count)

        def send(way, side, slot, lon, lat, out):
            copy(strips.at[way, rows], rims.at[side, slot, rows], lon, lat, cast_send.at[out],
                 cast_recv.at[which, 1 + side]).start()

        @pl.when(not_south)
        def _():
            around_lon(0, n_lon, lambda lon: send(0, 0, p, lon, q - 1, 1))

        @pl.when(not_pole)
        def _():
            around_lon(0, n_lon, lambda lon: send(1, 1, p, lon, q + 1, 2))

        @pl.when(at_pole)
        def _():
            around_lon(1, n_lon, lambda lon: send(1, 0, mirror, lon, q, 2))

    def cast_wait(which):
        first, count, size = parts[which]
        rows = pl.ds(first, count)
        drain(tiles.at[pl.ds(0, n_lon - 1), pl.ds(first * NI, size)], cast_recv.at[which, 0])

        @pl.when(at_pole)
        def _():
            drain(rims.at[0, pl.ds(0, n_lon - 1), rows], cast_recv.at[which, 1])

        @pl.when(not_pole)
        def _():
            drain(rims.at[0, pl.ds(0, n_lon), rows], cast_recv.at[which, 1])

        @pl.when(not_south)
        def _():
            drain(rims.at[1, pl.ds(0, n_lon), rows], cast_recv.at[which, 2])

    first_guess = sea_ref[...].astype(F32) * eta_ref[...]
    for i, x in enumerate((height, first_guess, drive_ref[...])):
        tiles[p, i * NI:(i + 1) * NI] = x
    pack_strips(0, 1.0, height, first_guess, drive_ref[...])
    cast(0)
    cast_strips(0)
    level_i = lane - K * (lane // K)
    level_l = level_i.astype(F32) + 0.5
    thick_l = zero
    for k in range(K):
        thick_l = jnp.where(level_i == k, thick_ref[k], thick_l)

    near_e = jnp.where(sub == NI - 1, 0.0, jnp.minimum(depth, pltpu.roll(depth, NI - 1, 0)))
    near_w = jnp.where(sub == 0, 0.0, jnp.minimum(depth, pltpu.roll(depth, 1, 0)))
    near_n = jnp.where(lane == NJ - 1, 0.0, jnp.minimum(depth, pltpu.roll(depth, NJ - 1, 1)))
    near_s = jnp.where(lane == 0, 0.0, jnp.minimum(depth, pltpu.roll(depth, 1, 1)))
    lat_index = (q * NJ + lane).astype(F32)
    coriolis = CORIOLIS * (2.0 * (lat_index + 0.5) / (n_lat * NJ) - 1.0)

    def gate(d, kf, x):
        return jnp.where(d > kf, x, 0.0)

    def inner_lap(x, kf):
        total = gate(near_e, kf, pltpu.roll(x, NI - 1, 0) - x) + gate(near_w, kf, pltpu.roll(x, 1, 0) - x)
        return total + (gate(near_n, kf, pltpu.roll(x, NJ - 1, 1) - x) + gate(near_s, kf, pltpu.roll(x, 1, 1) - x))

    def before_level(k, pc):
        kf = lax.convert_element_type(k, F32) + 0.5
        u, v = u_ref[k], v_ref[k]
        laps[0, k] = inner_lap(u, kf)
        laps[1, k] = inner_lap(v, kf)
        pc = pc + gate(depth, kf, (CONTRACTION * s_ref[k] - EXPANSION * t_ref[k]) * thick_ref[k])
        pressure[k] = pc
        grad_x = gate(near_e, kf, pltpu.roll(pc, NI - 1, 0) - pc) + gate(near_w, kf, pc - pltpu.roll(pc, 1, 0))
        grad_y = gate(near_n, kf, pltpu.roll(pc, NJ - 1, 1) - pc) + gate(near_s, kf, pc - pltpu.roll(pc, 1, 1))
        ou_ref[k] = u + coriolis * v - (0.5 * PRESSURE_SCALE) * grad_x
        ov_ref[k] = v - coriolis * u - (0.5 * PRESSURE_SCALE) * grad_y
        return pc

    def before_chunk(c, pc):
        for i in range(KC):
            pc = before_level(c * KC + i, pc)
        return pc

    lax.fori_loop(0, NC, before_chunk, zero)

    full = pl.ds(0, 2 * NI + 4)

    @pl.when(both_remote)
    def _():
        drain(pack_in.at[0, full], edge_sem.at[0])

    @pl.when(one_remote)
    def _():
        drain(pack_in.at[0, pl.ds(0, 2 * NI + 2)], edge_sem.at[0])

    @pl.when(not_south)
    def _():
        drain(pack_in.at[0, full], edge_sem.at[1])

    sign = jnp.where(lane >= 2 * K, -1.0, 1.0).astype(F32)

    def northern(slot, own):
        out = []
        for i in range(2):
            x = slots[slot, i]
            if own is not None:
                x = jnp.where(own, npk[i], x)
            out.append(jnp.where(at_pole, flip_rows(x) * sign, x))
        return out

    def southern(slot):
        return [jnp.where(not_south, slots[slot, i], 0.0) for i in range(2)]

    pn0, pn1 = northern(SLOT_N, None)
    pne0, pne1 = northern(SLOT_NE, ne_self)
    pnw0, pnw1 = northern(SLOT_NW, nw_self)
    ps0, ps1 = southern(SLOT_S)
    pse0, pse1 = southern(SLOT_SE)
    psw0, psw1 = southern(SLOT_SW)

    def shift_e(x, row):
        return jnp.where(sub == NI - 1, row, pltpu.roll(x, NI - 1, 0))

    def shift_w(x, row):
        return jnp.where(sub == 0, row, pltpu.roll(x, 1, 0))

    def wet_l(d):
        return jnp.where(level_l < d, 1.0, 0.0)

    def spread(x, i):
        return jnp.broadcast_to(x[:, i:i + 1], (NI, NJ))

    def packed_lap(c0, c1, e0, e1, w0, w1, own, own_depth):
        d = spread(c1, 0)
        de = shift_e(d, jnp.broadcast_to(e1[0:1, 0:1], (NI, NJ)))
        dw = shift_w(d, jnp.broadcast_to(w1[NI - 1:NI, 0:1], (NI, NJ)))
        xe = shift_e(c0, jnp.broadcast_to(e0[0:1, :], (NI, NJ)))
        xw = shift_w(c0, jnp.broadcast_to(w0[NI - 1:NI, :], (NI, NJ)))
        total = wet_l(de) * (xe - c0) + wet_l(dw) * (xw - c0)
        total = total + wet_l(spread(c1, 1)) * (c1 - c0) + wet_l(own_depth) * (own - c0)
        return wet_l(d) * total

    def packed_pressure(c0, c1):
        x = (CONTRACTION * pltpu.roll(c0, NJ - K, 1) - EXPANSION * c0) * thick_l * wet_l(spread(c1, 0))
        step = 1
        while step < K:
            x = x + jnp.where(level_i >= step, pltpu.roll(x, step, 1), 0.0)
            step *= 2
        return x

    lap_n = packed_lap(pn0, pn1, pne0, pne1, pnw0, pnw1, n0, spread(depth, NJ - 1))
    lap_s = packed_lap(ps0, ps1, pse0, pse1, psw0, psw1, s0, spread(depth, 0))
    rim[0] = pn0
    rim[1] = ps0
    rim[2] = lap_n
    rim[3] = lap_s
    rim[4] = packed_pressure(pn0, pn1)
    rim[5] = packed_pressure(ps0, ps1)

    drain(pack_in.at[:, BASE:REST], chunk_sem.at[NC])
    base_e = pack_in[0, BASE:BASE + 1, :]
    base_w = pack_in[1, BASE:BASE + 1, :]
    is_w = sub == 0
    is_s = lane == 0
    depth_ew = jnp.where(is_w, base_w, base_e)
    depth_ns = jnp.where(is_s, ps1, pltpu.roll(pn1, NJ - 1, 1))
    on_ew = jnp.logical_or(is_w, sub == NI - 1)
    on_ns = jnp.logical_or(is_s, lane == NJ - 1)
    near_ew = jnp.where(on_ew, jnp.minimum(depth, depth_ew), 0.0)
    near_ns = jnp.where(on_ns, jnp.minimum(depth, depth_ns), 0.0)
    scale_ew = jnp.where(is_w, 0.5 * PRESSURE_SCALE, -0.5 * PRESSURE_SCALE)
    scale_ns = jnp.where(is_s, 0.5 * PRESSURE_SCALE, -0.5 * PRESSURE_SCALE)

    def rim_ns(north, south, k):
        x = pltpu.roll(north, (NJ - 1 - k) % NJ, 1)
        return jnp.where(is_s, pltpu.roll(south, (NJ - k) % NJ, 1), x)

    def side_ew(c, row):
        row = c * SIDE + row
        return jnp.where(is_w, pack_in[1, row:row + 1, :], pack_in[0, row:row + 1, :])

    totals = [zero] * 2
    exports = [zero] * 2
    for c in range(NC):
        drain(pack_in.at[:, c * SIDE:(c + 1) * SIDE], chunk_sem.at[c])
        for i in range(KC):
            k = c * KC + i
            kf = k + 0.5
            h = thick_ref[k]
            pc = pressure[k]
            u_part = ou_ref[k] + scale_ew * gate(near_ew, kf, side_ew(c, 2 * KC + i) - pc)
            v_part = ov_ref[k] + scale_ns * gate(near_ns, kf, rim_ns(rim[4], rim[5], k) - pc)
            for m, (x, part, out) in enumerate(((u_ref[k], u_part, ou_ref), (v_ref[k], v_part, ov_ref))):
                at = (2 + m) * K + k
                lap = laps[m, k] + gate(near_ew, kf, side_ew(c, m * KC + i) - x)
                lap = lap + gate(near_ns, kf, rim_ns(rim[0], rim[1], at) - x)
                edge_lap = gate(near_ew, kf, lap)
                friction = inner_lap(lap, kf) - edge_lap
                friction = friction + gate(near_ns, kf, rim_ns(rim[2], rim[3], at) - lap)
                star = gate(depth, kf, part - FRICTION * friction)
                out[k] = star
                totals[m] = totals[m] + h * star
                exports[m] = exports[m] + h * edge_lap

    tiles[p, EARLY * NI:(EARLY + 1) * NI] = totals[0]
    tiles[p, (EARLY + 1) * NI:(EARLY + 2) * NI] = totals[1]
    exports = [-FRICTION * x for x in exports]
    for m in range(2):
        row = (EARLY + LATE) * NI + 2 * m
        tiles[p, row:row + 1] = exports[m][0:1]
        tiles[p, row + 1:row + 2] = exports[m][NI - 1:]
    cast(1)
    out_rows = zero
    for row, x in ((0, exports[0][0:1]), (1, exports[1][0:1]), (NI - 2, exports[1][NI - 1:]), (NI - 1, exports[0][NI - 1:])):
        out_rows = jnp.where(sub == row, jnp.broadcast_to(x, (NI, NJ)), out_rows)
    pack_strips(1, -1.0, totals[0], totals[1], out_rows)
    cast_strips(1)
    rest = pl.ds(REST, 4 * K)
    copy(pack_out.at[0, rest], pack_in.at[1, rest], east_dev, q, send_sem.at[0], chunk_sem.at[NC + 1]).start()
    copy(pack_out.at[1, rest], pack_in.at[0, rest], west_dev, q, send_sem.at[0], chunk_sem.at[NC + 1]).start()

    cast_wait(0)
    flat = tiles.reshape(n_lon * TILES * NI, NJ)
    flat_rim = rims.reshape(2 * n_lon * NI, NJ)
    lanes = iota((n_lon, NJ), 1)

    def loader(f):
        main = [flat[pl.ds(f * NI + s, n_lon, stride=TILES * NI), :] for s in range(NI)]
        north = flat_rim[pl.ds(f, n_lon, stride=NI), :]
        south = jnp.where(not_south, flat_rim[pl.ds(n_lon * NI + f, n_lon, stride=NI), :], 0.0)
        outer = []
        for s in range(NI):
            x = jnp.where(lanes >= NJ - width, pltpu.roll(south, (NJ - width - width * s) % NJ, 1), 0.0)
            outer.append(jnp.where(lanes < width, pltpu.roll(north, (NJ - width * s) % NJ, 1), x))
        return [main, outer]

    def late_wait():
        cast_wait(1)

    def share(total):
        sums[q] = jnp.broadcast_to(total, (NI, NJ))
        for r in range(1, n_lat):
            lat = lax.rem(q + r, n_lat)
            copy(sums.at[q], sums.at[q], p, lat, cast_send.at[3], cast_recv.at[2, 0]).start()

    x, slope_x, slope_y = surface_solve(loader, late_wait, share, n_lon, K, NI, NJ)
    for i, field in enumerate((x, slope_x, slope_y)):
        for s in range(NI):
            held[i, pl.ds(s, n_lon, stride=NI), :] = field[s]
    block = pl.ds(pl.multiple_of(p * NI, NI), NI)
    ox_ref[0] = held[0, block, :]
    slope_u = GRAVITY * held[1, block, :]
    slope_v = GRAVITY * held[2, block, :]
    drain(pack_in.at[:, rest], chunk_sem.at[NC + 1])
    turned = zero
    for i, row in enumerate((pne0[0:1], pse0[0:1], pnw0[NI - 1:], psw0[NI - 1:])):
        turned = jnp.where(sub == i, jnp.broadcast_to(row, (NI, NJ)), turned)
    turned = flip_lanes(turned)
    after = pltpu.roll(turned, 1, 1)
    corners = ((wide(turned[0:1]), wide(after[1:2])), (wide(turned[2:3]), wide(after[3:4])))
    corner_depths = ((pne1[0:1], pse1[0:1]), (pnw1[NI - 1:], psw1[NI - 1:]))
    side_depths = []
    for side, d1 in enumerate((NI - 1, 0)):
        base = pack_in[side, BASE:REST, :]
        cn1, cs1 = corner_depths[side]
        d = wide(base[0:1, :])
        dn = jnp.where(lane_c == NJ - 1, jnp.broadcast_to(cn1[:, 0:1], (KC, NJ)), pltpu.roll(d, NJ - 1, 1))
        ds = jnp.where(lane_c == 0, jnp.broadcast_to(cs1[:, 0:1], (KC, NJ)), pltpu.roll(d, 1, 1))
        own = wide(depth[d1:d1 + 1, :])
        side_depths.append([jnp.minimum(d, o) for o in (wide(base[1:2, :]), own, dn, ds)])

    for c in range(NC):
        level_c = row_c.astype(F32) + (c * KC + 0.5)

        def part(d, x):
            return jnp.where(level_c < d, x, 0.0)

        for side in range(2):
            far, own, dn, ds = side_depths[side]
            cn0, cs0 = corners[side]
            for m in range(2):
                row = c * SIDE + m * KC
                outer = REST + (2 + m) * K + c * KC
                x = pack_in[side, row:row + KC, :]
                at = (2 + m) * K + c * KC
                cn = pltpu.roll(cn0, at, 1, stride=1, stride_axis=0)
                cs = pltpu.roll(cs0, at, 1, stride=1, stride_axis=0)
                xn = jnp.where(lane_c == NJ - 1, cn, pltpu.roll(x, NJ - 1, 1))
                xs = jnp.where(lane_c == 0, cs, pltpu.roll(x, 1, 1))
                total = part(far, pack_in[side, outer:outer + KC, :] - x)
                total = total + part(own, pack_out[side, row:row + KC, :] - x)
                side_lap[c, 2 * side + m] = total + (part(dn, xn - x) + part(ds, xs - x))

    both_e = jnp.minimum(depth, shift_e(depth, base_e))
    both_w = jnp.minimum(depth, shift_w(depth, base_w))
    both_n = jnp.where(lane == NJ - 1, near_ns, near_n)
    both_s = jnp.where(is_s, near_ns, near_s)

    def shift_n(x, packed, source):
        return jnp.where(lane == NJ - 1, pltpu.roll(packed, NJ - 1 - source, 1), pltpu.roll(x, NJ - 1, 1))

    def shift_s(x, packed, source):
        return jnp.where(lane == 0, pltpu.roll(packed, lax.rem(NJ - source, NJ), 1), pltpu.roll(x, 1, 1))

    def around(c, inner, ref, f):
        k = c * KC + inner
        x = ref[k]
        row = pl.ds(c * SIDE + (f - 2) * KC + inner if f >= 2 else REST + f * K + k, 1)
        return (x, shift_e(x, pack_in[0, row, :]), shift_w(x, pack_in[1, row, :]),
                shift_n(x, rim[0], f * K + k), shift_s(x, rim[1], f * K + k))

    def tracers(c, i, carry):
        inner = pl.ds(i, 1)
        k = c * KC + i
        flux_t, flux_s = carry
        kf = lax.convert_element_type(k, F32) + 0.5
        h = thick_ref[k]
        nxt = jnp.minimum(k + 1, K - 1)
        h_next = thick_ref[nxt]
        hv = jnp.full((NI, NJ), h, F32)
        inv_space = 1.0 / (0.5 * (hv + h_next))
        inv_h = MIXING / hv

        def wet(d):
            return jnp.where(d > kf, 1.0, 0.0)

        mc = wet(depth)
        me, mw, mn, ms = wet(both_e), wet(both_w), wet(both_n), wet(both_s)
        below = jnp.where(jnp.logical_and(depth > kf + 1.0, k < K - 1), inv_space, 0.0)
        t = around(c, i, t_ref, 0)
        s = around(c, i, s_ref, 1)
        u0, ue, uw = around(c, i, u_ref, 2)[:3]
        v0, _, _, vn, vs = around(c, i, v_ref, 3)
        ae = 0.25 * me * (u0 + ue)
        aw = 0.25 * mw * (u0 + uw)
        an = 0.25 * mn * (v0 + vn)
        as_ = 0.25 * ms * (v0 + vs)
        ge, gw, gn, gs = DIFFUSION * me, DIFFUSION * mw, DIFFUSION * mn, DIFFUSION * ms

        def tracer(x, ref, flux_above):
            c, e, w, n, so = x
            total = aw * (w + c) - gw * (c - w) - ae * (c + e) + ge * (e - c)
            total = total + as_ * (so + c) - gs * (c - so) - an * (c + n) + gn * (n - c)
            flux = below * (ref[nxt] - c)
            return mc * (c + total + inv_h * (flux - flux_above)), flux

        new_t, flux_t = tracer(t, t_ref, flux_t)
        new_s, flux_s = tracer(s, s_ref, flux_s)
        ot_ref[k] = new_t
        os_ref[k] = new_s
        for m, (out, slope) in enumerate(((ou_ref, slope_u), (ov_ref, slope_v))):
            lap_ew = jnp.where(is_w, side_lap[c, 2 + m, inner, :], side_lap[c, m, inner, :])
            star = out[k] - FRICTION * gate(near_ew, kf, lap_ew)
            out[k] = gate(depth, kf, star - slope)
        return flux_t, flux_s

    def tracer_chunk(c, carry):
        for i in range(KC):
            carry = tracers(c, i, carry)
        return carry

    lax.fori_loop(0, NC, tracer_chunk, (zero,) * 2)

    drain(pack_out, send_sem.at[0])

    @pl.when(not_south)
    def _():
        drain(pack_in.at[0, full], send_sem.at[1])

    @pl.when(both_remote)
    def _():
        drain(pack_in.at[0, full], send_sem.at[2])

    @pl.when(one_remote)
    def _():
        drain(pack_in.at[0, pl.ds(0, 2 * NI + 2)], send_sem.at[2])

    used = pl.ds(0, TILES)
    drain(tiles.at[pl.ds(0, n_lon - 1), pl.ds(0, (EARLY + LATE) * NI + 4)], cast_send.at[0])

    @pl.when(not_south)
    def _():
        drain(rims.at[0, pl.ds(0, n_lon), used], cast_send.at[1])

    @pl.when(not_pole)
    def _():
        drain(rims.at[0, pl.ds(0, n_lon), used], cast_send.at[2])

    @pl.when(at_pole)
    def _():
        drain(rims.at[0, pl.ds(0, n_lon - 1), used], cast_send.at[2])

    drain(sums.at[pl.ds(0, n_lat - 1)], cast_recv.at[2, 0])
    total = functools.reduce(lambda a, b: a + b, [sums[lat] for lat in range(n_lat)])
    ox_ref[1] = jnp.sqrt(total / (n_lon * NI * n_lat * NJ) + EPSILON)
    drain(sums.at[pl.ds(0, n_lat - 1)], cast_send.at[3])


def surface_solve(load, late_wait, share, n_lon, K, NI, NJ):
    tiles = range(2)
    lines = range(NI)
    lane = iota((n_lon, NJ), 1)

    def every(fn, *arrays):
        return [[fn(*(a[b][s] for a in arrays)) for s in lines] for b in tiles]

    def east(x):
        return [x[b][1:] + [pltpu.roll(x[b][0], n_lon - 1, 0)] for b in tiles]

    def west(x):
        return [[pltpu.roll(x[b][NI - 1], 1, 0)] + x[b][:-1] for b in tiles]

    def joined(x, shift, edge):
        moved = [[pltpu.roll(x[b][s], shift, 1) for s in lines] for b in tiles]
        return [[jnp.where(lane == edge, moved[1 - b][s], moved[b][s]) for s in lines] for b in tiles]

    def north(x):
        return joined(x, NJ - 1, NJ - 1)

    def south(x):
        return joined(x, 1, 0)

    height = load(0)
    scale = lambda a, c: jnp.minimum(a, c) * (1.0 / K)
    w_e = every(scale, height, east(height))
    w_w = every(scale, height, west(height))
    w_n = every(scale, height, north(height))
    w_s = every(scale, height, south(height))
    diag = every(lambda a, b, c, d: STORAGE + a + b + c + d, w_e, w_w, w_n, w_s)

    def apply(x):
        return every(
            lambda dg, c, we, e, ww, w, wn, n, ws, s: dg * c - (we * e + ww * w + wn * n + ws * s),
            diag, x, w_e, east(x), w_w, west(x), w_n, north(x), w_s, south(x))

    middle = NI // 2
    spans = [(s, s - 1, s + 1) for s in range(middle)]
    spans += [(s, s + 1, s - 1) for s in range(NI - 1, middle - 1, -1)]
    pivots, carries, factors = ([[None] * NI for _ in tiles] for _ in range(3))
    joints = []
    for b in tiles:
        for s, before, after in spans:
            back, ahead = (w_w, w_e) if after > s else (w_e, w_w)
            pivot = diag[b][s]
            if s not in (0, NI - 1):
                pivot = pivot + back[b][s] * factors[b][before]
            pivots[b][s] = 1.0 / pivot
            carries[b][s] = back[b][s] * pivots[b][s]
            factors[b][s] = -ahead[b][s] * pivots[b][s]
        joints.append(1.0 / (1.0 - factors[b][middle - 1] * factors[b][middle]))

    def precondition(r):
        out = []
        for b in tiles:
            part = [None] * NI
            for s, before, after in spans:
                part[s] = r[b][s] * pivots[b][s]
                if s not in (0, NI - 1):
                    part[s] = part[s] + carries[b][s] * part[before]
            low, high = part[middle - 1], part[middle]
            part[middle - 1] = (low - factors[b][middle - 1] * high) * joints[b]
            part[middle] = (high - factors[b][middle] * low) * joints[b]
            for s in range(middle - 2, -1, -1):
                part[s] = part[s] - factors[b][s] * part[s + 1]
            for s in range(middle + 1, NI):
                part[s] = part[s] - factors[b][s] * part[s - 1]
            out.append(part)
        return out

    x = load(1)
    drive = load(2)
    start = every(lambda h, d, a: jnp.where(h > 0.0, d, 0.0) - a, height, drive, apply(x))
    late_wait()
    t_u = load(EARLY)
    t_v = load(EARLY + 1)
    inner, outer = load(EARLY + LATE)
    for m, t in enumerate((t_u, t_v)):
        for b, (from_w, from_e) in enumerate(((inner[2 * m], inner[2 * m + 1]), (outer[m], outer[NI - 1 - m]))):
            t[b][NI - 1] = t[b][NI - 1] + pltpu.roll(from_w, n_lon - 1, 0)
            t[b][0] = t[b][0] + pltpu.roll(from_e, 1, 0)
    residual = every(
        lambda h, d, e, w, n, s: d - jnp.where(h > 0.0, 0.5 * DIVERGENCE * ((e - w) + (n - s)), 0.0),
        height, start, east(t_u), west(t_u), north(t_v), south(t_v))
    mid = 0.5 * (SPECTRUM_HIGH + SPECTRUM_LOW)
    half = 0.5 * (SPECTRUM_HIGH - SPECTRUM_LOW)
    ratio = mid / half
    direction = every(lambda a: a / mid, precondition(residual))
    rho = 1.0 / ratio
    for step in range(ITERS):
        x = every(lambda a, b: a + b, x, direction)
        residual = every(lambda a, b: a - b, residual, apply(direction))
        if step + 1 < ITERS:
            rho_next = 1.0 / (2.0 * ratio - rho)
            keep, gain = rho_next * rho, 2.0 * rho_next / half
            direction = every(lambda d, z: keep * d + gain * z, direction, precondition(residual))
            rho = rho_next
    squares = functools.reduce(lambda a, b: a + b, [a * a for a in residual[0]])
    share(jnp.sum(jnp.sum(squares, axis=1, keepdims=True), axis=0, keepdims=True))
    slope_x = every(lambda e, w: 0.5 * (e - w), east(x), west(x))
    slope_y = every(lambda n, s: 0.5 * (n - s), north(x), south(x))
    return x[0], slope_x[0], slope_y[0]


def finish_kernel(kept, x_ref, ot_ref, os_ref, ou_ref, ov_ref, ox_ref, orms_ref, rms, sem):
    for f, target in enumerate((ot_ref, os_ref, ou_ref, ov_ref)):
        pltpu.make_async_copy(kept.at[f], target, sem.at[0]).start()
    surface = pltpu.make_async_copy(x_ref.at[0], ox_ref, sem.at[1])
    surface.start()
    rms[0] = jnp.max(x_ref[1])
    scalar = pltpu.make_async_copy(rms, orms_ref, sem.at[2])
    scalar.start()
    pltpu.make_async_copy(kept, kept, sem.at[0]).wait()
    surface.wait()
    scalar.wait()


def per_device(n_lon, n_lat, *args):
    K, NI, NJ = args[0].shape
    KC = 8 if K % 8 == 0 else K
    NC = K // KC
    vmem = pl.BlockSpec(memory_space=pltpu.VMEM)
    hbm = pl.BlockSpec(memory_space=pltpu.HBM)
    big = jax.ShapeDtypeStruct((K, NI, NJ), F32)
    tile = jax.ShapeDtypeStruct((NI, NJ), F32)
    one = jax.ShapeDtypeStruct((1,), F32)
    pack = pltpu.VMEM((2, 7 * K + NI, NJ), F32)

    def room(*lead):
        return pltpu.VMEM((*lead, NI, NJ), F32)

    parts = pl.pallas_call(
        functools.partial(step_kernel, n_lon, n_lat, KC),
        out_shape=(room(4, K), room(2)),
        in_specs=[hbm] * 9,
        out_specs=(vmem,) * 2,
        scratch_shapes=[
            room(4, K), pltpu.VMEM((2, NI, NJ), jnp.int32), room(2), pltpu.SMEM((K,), F32),
            pack, pack, room(2, 2), room(6, 2), room(6), pltpu.VMEM((NC, 4, KC, NJ), F32),
            room(2, K), room(K), pltpu.VMEM((n_lon, TILES * NI, NJ), F32), room(2), room(2, n_lon), room(n_lat),
            pltpu.VMEM((3, n_lon * NI, NJ), F32),
            pltpu.SemaphoreType.DMA((3,)), pltpu.SemaphoreType.DMA((3,)), pltpu.SemaphoreType.DMA((NC + 2,)),
            pltpu.SemaphoreType.DMA((2,)), pltpu.SemaphoreType.DMA((4,)), pltpu.SemaphoreType.DMA((3, 3)),
        ],
        compiler_params=pltpu.CompilerParams(
            collective_id=0, has_side_effects=True),
        name="step",
    )(*args)
    outs = pl.pallas_call(
        finish_kernel,
        out_shape=(big, big, big, big, tile, one),
        in_specs=[vmem] * 2,
        out_specs=(hbm,) * 6,
        scratch_shapes=[pltpu.SMEM((1,), F32), pltpu.SemaphoreType.DMA((3,))],
        name="finish",
    )(*[pltpu.with_memory_space_constraint(part, pltpu.VMEM) for part in parts])
    return outs[:5] + (outs[5].reshape(()),)


def solution(mesh):
    n_lon, n_lat = mesh.shape["lon"], mesh.shape["lat"]
    spec3 = P(None, "lon", "lat")
    spec2 = P("lon", "lat")
    return jax.shard_map(
        functools.partial(per_device, n_lon, n_lat),
        mesh=mesh,
        in_specs=(spec3, spec3, spec3, spec3, spec2, spec2, P(), spec2, spec2),
        out_specs=(spec3, spec3, spec3, spec3, spec2, P()),
        check_vma=False,
    )
```

time: 25.1 us -> 22.6 us (0.900)
  Pallas kernels: 24.3 us -> 21.8 us
    pallas_call x1, Pallas kernels: 22.9 us -> 20.9 us  [per_device(): pl.pallas_call(functools.partial(step_kernel, n_lon, n_lat, KC), out_shap...]
    pallas_call x1, Pallas kernels: 1.4 us -> 0.82 us  [per_device(): pl.pallas_call(finish_kernel, out_shape=(big, big, big, big, tile, one),...]
where the time goes in v1:
time: 22.6 us; the launch traced here: 22.4 us
  Pallas kernels  21.8 us (96%)
  between operations  0.64 us (3%)
    pallas_call x1, Pallas kernels, per_device(): pl.pallas_call(functools.partial(step_kernel, n_lon, n_lat, KC), out_shap...  20.9 us
    pallas_call x1, Pallas kernels, per_device(): pl.pallas_call(finish_kernel, out_shape=(big, big, big, big, tile, one),...  0.82 us

profile of v1, /device:TPU:0, one launch (start us, length us, event | category | flops | bytes accessed | tf_op | source)
XLA Modules:
  0.0 22.4 jit_solution(16759990011193707483)
XLA Ops:
  0.6 20.9 %step.1 = (f32[4,32,8,128]{3,2,1,0:T(8,128)S(1)}, f32[2,8,128]{2,1,0:T(8,128)S(1)}) custom-call(f32[32,8,128]{2,1,0:T(8,128)} %refs_0_.1, f32[32,8,128]{2,1,0:T(8,128)} %refs_1_.1, f32[32,8,128]{2,1,0:T(8,128)} %refs_2_.1, f32[32,8,128]{2,1,0:T(8,128)} %refs_3_.1, s32[8,128]{1,0:T(8,128)} %refs_4_.1, s32[8,128]{1,0:T(8,128)} %refs_5_.1, f32[32]{0:T(128)} %refs_6_.1, ...), custom_call_target="tpu_custom_call" | custom-call | tf_op jit(solution)/shard_map/step/pallas_call | solution.py:827
  21.6 0.8 %finish.1 = (f32[32,8,128]{2,1,0:T(8,128)}, f32[32,8,128]{2,1,0:T(8,128)}, f32[32,8,128]{2,1,0:T(8,128)}, f32[32,8,128]{2,1,0:T(8,128)}, f32[8,128]{1,0:T(8,128)}, /*index=5*/f32[1]{0:T(128)}) custom-call(f32[4,32,8,128]{3,2,1,0:T(8,128)S(1)} %get-tuple-element.14.kept, f32[2,8,128]{2,1,0:T(8,128)S(1)} %get-tuple-element.15.x_ref), custom_call_target="tpu_custom_call" | custom-call | tf_op jit(solution)/shard_map/finish/pallas_call | solution.py:844

commit v2 on v1

--- a/solution.py
+++ b/solution.py
@@ -24,7 +24,6 @@
 
 MESH = pl.DeviceIdType.MESH
 F32 = jnp.float32
-SLOT_N, SLOT_NE, SLOT_NW, SLOT_S, SLOT_SE, SLOT_SW = range(6)
 EARLY = 3
 LATE = 2
 TILES = EARLY + LATE + 1
@@ -60,13 +59,12 @@
 def step_kernel(n_lon, n_lat, KC, *refs):
     sources, refs = refs[:9], refs[9:]
     (kept, ox_ref), refs = refs[:2], refs[2:]
-    (fields, ints, floats, thick_ref, pack_out, pack_in, edges, slots, rim, side_lap, laps, pressure, tiles, strips,
+    (fields, ints, floats, thick_ref, pack_out, pack_in, edges, slots, lap_edges, lap_slots, rim, laps, pressure, tiles, strips,
      rims, sums, held, load_sem, send_sem, chunk_sem, edge_sem, cast_send, cast_recv) = refs
     _, K, NI, NJ = fields.shape
     NC = K // KC
     SIDE = 3 * KC
-    BASE = NC * SIDE
-    REST = BASE + NI
+    REST = NI + NC * SIDE
     t_ref, s_ref, u_ref, v_ref = (fields.at[f] for f in range(4))
     ot_ref, os_ref, ou_ref, ov_ref = (kept.at[f] for f in range(4))
     num_ref, sea_ref, eta_ref, drive_ref = ints.at[0], ints.at[1], floats.at[0], floats.at[1]
@@ -78,14 +76,7 @@
     not_pole = q < n_lat - 1
     not_south = q > 0
     mirror = n_lon - 1 - p
-    mirror_ne = lax.rem(2 * n_lon - 2 - p, n_lon)
-    mirror_nw = lax.rem(2 * n_lon - p, n_lon)
-    ne_remote = jnp.logical_or(not_pole, mirror_ne != p)
-    nw_remote = jnp.logical_or(not_pole, mirror_nw != p)
-    both_remote = jnp.logical_and(ne_remote, nw_remote)
-    one_remote = jnp.logical_not(both_remote)
-    ne_self = jnp.logical_and(at_pole, mirror_ne == p)
-    nw_self = jnp.logical_and(at_pole, mirror_nw == p)
+    lons = [lax.rem(p + r, n_lon) for r in range(min(n_lon, 8))]
 
     barrier = pltpu.get_barrier_semaphore()
 
@@ -101,9 +92,9 @@
             fn(lax.rem(p + r, n_lon))
             return carry
 
-        if last - first <= 8:
-            for r in range(first, last):
-                visit(r, 0)
+        if n_lon <= 8:
+            for lon in lons[first:last]:
+                fn(lon)
         else:
             lax.fori_loop(first, last, visit, 0)
 
@@ -162,12 +153,12 @@
     def wide(row):
         return jnp.broadcast_to(row, (KC, NJ))
 
-    for side, (d1, d2) in enumerate(((NI - 1, NI - 2), (0, 1))):
+    for side, d1 in enumerate((NI - 1, 0)):
         own_depth = wide(depth[d1:d1 + 1, :])
         carried = jnp.zeros((KC, NJ), F32)
         for c in range(NC):
             levels = slice(c * KC, (c + 1) * KC)
-            row = c * SIDE
+            row = NI + c * SIDE
             pack_out[side, row:row + KC, :] = u_ref[levels, d1, :]
             pack_out[side, row + KC:row + 2 * KC, :] = v_ref[levels, d1, :]
             t_col, s_col = t_ref[levels, d1, :], s_ref[levels, d1, :]
@@ -180,13 +171,10 @@
             x = x + carried
             pack_out[side, row + 2 * KC:row + 3 * KC, :] = x
             carried = wide(x[KC - 1:KC, :])
-            for f, (ref, d) in enumerate(((u_ref, d2), (v_ref, d2))):
-                row = REST + (2 + f) * K + c * KC
-                pack_out[side, row:row + KC, :] = ref[levels, d, :]
             for f, x in enumerate((t_col, s_col)):
                 row = REST + f * K + c * KC
                 pack_out[side, row:row + KC, :] = x
-        pack_out[side, BASE:REST, :] = jnp.where(sub == 0, depth[d1:d1 + 1, :], depth[d2:d2 + 1, :])
+        pack_out[side, 0:NI, :] = jnp.broadcast_to(depth[d1:d1 + 1, :], (NI, NJ))
 
     zero = jnp.zeros((NI, NJ), F32)
 
@@ -194,23 +182,16 @@
         moved = pltpu.roll(x, (target - source) % NJ, 1) if source != target else x
         return jnp.where(lane == target, moved, acc)
 
-    n0 = s0 = n1 = s1 = zero
+    n0 = s0 = zero
     for f, ref in enumerate((t_ref, s_ref, u_ref, v_ref)):
         for k in range(K):
-            x = ref[k]
-            target = f * K + k
-            n0 = put(n0, x, NJ - 1, target)
-            s0 = put(s0, x, 0, target)
-            if f >= 2:
-                n1 = put(n1, x, NJ - 2, target)
-                s1 = put(s1, x, 1, target)
-    n1 = put(put(n1, depth, NJ - 1, 0), depth, NJ - 2, 1)
-    s1 = put(put(s1, depth, 0, 0), depth, 1, 1)
+            n0 = put(n0, ref[k], NJ - 1, f * K + k)
+            s0 = put(s0, ref[k], 0, f * K + k)
     npk, spk = edges.at[0], edges.at[1]
     npk[0] = n0
-    npk[1] = n1
+    npk[1] = put(zero, depth, NJ - 1, 0)
     spk[0] = s0
-    spk[1] = s1
+    spk[1] = put(zero, depth, 0, 0)
 
     peers = n_lon + n_lat - 2 + (n_lon - 1) * (not_south.astype(jnp.int32) + not_pole.astype(jnp.int32))
     pl.semaphore_wait(barrier, peers)
@@ -220,57 +201,47 @@
             src_ref=src, dst_ref=dst, send_sem=out, recv_sem=into,
             device_id={"lon": lon, "lat": lat}, device_id_type=MESH)
 
-    def edge(src, slot, lon, lat, out, row=None):
-        dst = slots.at[slot]
-        if slot in (SLOT_NE, SLOT_SE, SLOT_NW, SLOT_SW):
-            if row is None:
-                row = 0 if slot in (SLOT_NE, SLOT_SE) else NI - 1
-            src, dst = src.at[:, row:row + 1, :], dst.at[:, row:row + 1, :]
-        into = 0 if slot in (SLOT_N, SLOT_NE, SLOT_NW) else 1
-        copy(src, dst, lon, lat, send_sem.at[out], edge_sem.at[into]).start()
-
-    @pl.when(at_pole)
-    def _():
-        edge(npk, SLOT_N, mirror, q, 2)
-
-    @pl.when(jnp.logical_and(at_pole, mirror_ne != p))
-    def _():
-        edge(npk, SLOT_NE, mirror_ne, q, 2, NI - 1)
-
-    @pl.when(jnp.logical_and(at_pole, mirror_nw != p))
-    def _():
-        edge(npk, SLOT_NW, mirror_nw, q, 2, 0)
-
-    @pl.when(not_south)
-    def _():
-        edge(spk, SLOT_NW, east_dev, q - 1, 1)
-        edge(spk, SLOT_NE, west_dev, q - 1, 1)
-        edge(spk, SLOT_N, p, q - 1, 1)
-
-    @pl.when(not_pole)
-    def _():
-        edge(npk, SLOT_SW, east_dev, q + 1, 2)
-        edge(npk, SLOT_SE, west_dev, q + 1, 2)
-        edge(npk, SLOT_S, p, q + 1, 2)
+    def meet(pack, slot, sem):
+        @pl.when(at_pole)
+        def _():
+            copy(pack.at[0], slot.at[0], mirror, q, send_sem.at[2], edge_sem.at[sem]).start()
+
+        @pl.when(not_south)
+        def _():
+            copy(pack.at[1], slot.at[0], p, q - 1, send_sem.at[1], edge_sem.at[sem]).start()
+
+        @pl.when(not_pole)
+        def _():
+            copy(pack.at[0], slot.at[1], p, q + 1, send_sem.at[2], edge_sem.at[sem + 1]).start()
+
+    def met(slot, sem):
+        drain(slot.at[0], edge_sem.at[sem])
+
+        @pl.when(not_south)
+        def _():
+            drain(slot.at[1], edge_sem.at[sem + 1])
+
+    meet(edges, slots, 0)
 
     def sides(first, rows, sem):
         rows = pl.ds(first, rows)
         copy(pack_out.at[0, rows], pack_in.at[1, rows], east_dev, q, send_sem.at[0], chunk_sem.at[sem]).start()
         copy(pack_out.at[1, rows], pack_in.at[0, rows], west_dev, q, send_sem.at[0], chunk_sem.at[sem]).start()
 
-    sides(BASE, NI, NC)
+    starts = [0] + [NI + c * SIDE for c in range(1, NC + 1)]
     for c in range(NC):
-        sides(c * SIDE, SIDE, c)
+        sides(starts[c], starts[c + 1] - starts[c], c)
 
     height = zero
     for k in range(K):
         height = height + jnp.where(depth > k + 0.5, thick_ref[k], 0.0)
     width = NJ // NI
     in_block = lane // width == sub
-    parts = ((0, EARLY, EARLY * NI), (EARLY, LATE + 1, LATE * NI + 4))
-
-    def pack_strips(which, sign, *arrays):
+    parts = ((0, EARLY, EARLY * NI), (EARLY, LATE + 3, LATE * NI + 6))
+
+    def pack_strips(which, sign, arrays, rows=()):
         first, count, _ = parts[which]
+        given = len(arrays)
         south = zero
         north = zero
         for i, x in enumerate(arrays):
@@ -282,7 +253,11 @@
                     north = jnp.where(sub == i, row, north)
                 else:
                     south = jnp.where(sub == i, row, south)
-        north = jnp.where(at_pole, sign * flip_lanes(north), north)
+        for i, row in enumerate(rows):
+            north = jnp.where(sub == given + i, row, north)
+            south = jnp.where(sub == given + i, row, south)
+        turned = jnp.where(sub >= given, pltpu.roll(north, width, 1), north) if rows else north
+        north = jnp.where(at_pole, sign * flip_lanes(turned), north)
         rows = slice(first, first + count)
         strips[0, rows] = south[:count]
         strips[1, rows] = north[:count]
@@ -336,7 +311,7 @@
     first_guess = sea_ref[...].astype(F32) * eta_ref[...]
     for i, x in enumerate((height, first_guess, drive_ref[...])):
         tiles[p, i * NI:(i + 1) * NI] = x
-    pack_strips(0, 1.0, height, first_guess, drive_ref[...])
+    pack_strips(0, 1.0, (height, first_guess, drive_ref[...]))
     cast(0)
     cast_strips(0)
     level_i = lane - K * (lane // K)
@@ -379,40 +354,16 @@
 
     lax.fori_loop(0, NC, before_chunk, zero)
 
-    full = pl.ds(0, 2 * NI + 4)
-
-    @pl.when(both_remote)
-    def _():
-        drain(pack_in.at[0, full], edge_sem.at[0])
-
-    @pl.when(one_remote)
-    def _():
-        drain(pack_in.at[0, pl.ds(0, 2 * NI + 2)], edge_sem.at[0])
-
-    @pl.when(not_south)
-    def _():
-        drain(pack_in.at[0, full], edge_sem.at[1])
+    met(slots, 0)
 
     sign = jnp.where(lane >= 2 * K, -1.0, 1.0).astype(F32)
 
-    def northern(slot, own):
-        out = []
-        for i in range(2):
-            x = slots[slot, i]
-            if own is not None:
-                x = jnp.where(own, npk[i], x)
-            out.append(jnp.where(at_pole, flip_rows(x) * sign, x))
-        return out
-
-    def southern(slot):
-        return [jnp.where(not_south, slots[slot, i], 0.0) for i in range(2)]
-
-    pn0, pn1 = northern(SLOT_N, None)
-    pne0, pne1 = northern(SLOT_NE, ne_self)
-    pnw0, pnw1 = northern(SLOT_NW, nw_self)
-    ps0, ps1 = southern(SLOT_S)
-    pse0, pse1 = southern(SLOT_SE)
-    psw0, psw1 = southern(SLOT_SW)
+    def arrived(slot, i, fold):
+        north = jnp.where(at_pole, flip_rows(slot[0, i]) * fold, slot[0, i])
+        return north, jnp.where(not_south, slot[1, i], 0.0)
+
+    pn0, ps0 = arrived(slots, 0, sign)
+    pn1, ps1 = arrived(slots, 1, 1.0)
 
     def shift_e(x, row):
         return jnp.where(sub == NI - 1, row, pltpu.roll(x, NI - 1, 0))
@@ -425,16 +376,6 @@
 
     def spread(x, i):
         return jnp.broadcast_to(x[:, i:i + 1], (NI, NJ))
-
-    def packed_lap(c0, c1, e0, e1, w0, w1, own, own_depth):
-        d = spread(c1, 0)
-        de = shift_e(d, jnp.broadcast_to(e1[0:1, 0:1], (NI, NJ)))
-        dw = shift_w(d, jnp.broadcast_to(w1[NI - 1:NI, 0:1], (NI, NJ)))
-        xe = shift_e(c0, jnp.broadcast_to(e0[0:1, :], (NI, NJ)))
-        xw = shift_w(c0, jnp.broadcast_to(w0[NI - 1:NI, :], (NI, NJ)))
-        total = wet_l(de) * (xe - c0) + wet_l(dw) * (xw - c0)
-        total = total + wet_l(spread(c1, 1)) * (c1 - c0) + wet_l(own_depth) * (own - c0)
-        return wet_l(d) * total
 
     def packed_pressure(c0, c1):
         x = (CONTRACTION * pltpu.roll(c0, NJ - K, 1) - EXPANSION * c0) * thick_l * wet_l(spread(c1, 0))
@@ -444,18 +385,14 @@
             step *= 2
         return x
 
-    lap_n = packed_lap(pn0, pn1, pne0, pne1, pnw0, pnw1, n0, spread(depth, NJ - 1))
-    lap_s = packed_lap(ps0, ps1, pse0, pse1, psw0, psw1, s0, spread(depth, 0))
     rim[0] = pn0
     rim[1] = ps0
-    rim[2] = lap_n
-    rim[3] = lap_s
-    rim[4] = packed_pressure(pn0, pn1)
-    rim[5] = packed_pressure(ps0, ps1)
-
-    drain(pack_in.at[:, BASE:REST], chunk_sem.at[NC])
-    base_e = pack_in[0, BASE:BASE + 1, :]
-    base_w = pack_in[1, BASE:BASE + 1, :]
+    rim[2] = packed_pressure(pn0, pn1)
+    rim[3] = packed_pressure(ps0, ps1)
+
+    drain(pack_in.at[:, 0:starts[1]], chunk_sem.at[0])
+    base_e = pack_in[0, 0:1, :]
+    base_w = pack_in[1, 0:1, :]
     is_w = sub == 0
     is_s = lane == 0
     depth_ew = jnp.where(is_w, base_w, base_e)
@@ -472,31 +409,35 @@
         return jnp.where(is_s, pltpu.roll(south, (NJ - k) % NJ, 1), x)
 
     def side_ew(c, row):
-        row = c * SIDE + row
+        row = NI + c * SIDE + row
         return jnp.where(is_w, pack_in[1, row:row + 1, :], pack_in[0, row:row + 1, :])
 
     totals = [zero] * 2
     exports = [zero] * 2
+    exports_ns = [zero] * 2
     for c in range(NC):
-        drain(pack_in.at[:, c * SIDE:(c + 1) * SIDE], chunk_sem.at[c])
+        if c:
+            drain(pack_in.at[:, starts[c]:starts[c + 1]], chunk_sem.at[c])
         for i in range(KC):
             k = c * KC + i
             kf = k + 0.5
             h = thick_ref[k]
             pc = pressure[k]
             u_part = ou_ref[k] + scale_ew * gate(near_ew, kf, side_ew(c, 2 * KC + i) - pc)
-            v_part = ov_ref[k] + scale_ns * gate(near_ns, kf, rim_ns(rim[4], rim[5], k) - pc)
+            v_part = ov_ref[k] + scale_ns * gate(near_ns, kf, rim_ns(rim[2], rim[3], k) - pc)
             for m, (x, part, out) in enumerate(((u_ref[k], u_part, ou_ref), (v_ref[k], v_part, ov_ref))):
                 at = (2 + m) * K + k
                 lap = laps[m, k] + gate(near_ew, kf, side_ew(c, m * KC + i) - x)
                 lap = lap + gate(near_ns, kf, rim_ns(rim[0], rim[1], at) - x)
                 edge_lap = gate(near_ew, kf, lap)
-                friction = inner_lap(lap, kf) - edge_lap
-                friction = friction + gate(near_ns, kf, rim_ns(rim[2], rim[3], at) - lap)
+                laps[m, k] = lap
+                edge_ns = gate(near_ns, kf, lap)
+                friction = inner_lap(lap, kf) - edge_lap - edge_ns
                 star = gate(depth, kf, part - FRICTION * friction)
                 out[k] = star
                 totals[m] = totals[m] + h * star
                 exports[m] = exports[m] + h * edge_lap
+                exports_ns[m] = exports_ns[m] + h * edge_ns
 
     tiles[p, EARLY * NI:(EARLY + 1) * NI] = totals[0]
     tiles[p, (EARLY + 1) * NI:(EARLY + 2) * NI] = totals[1]
@@ -505,15 +446,32 @@
         row = (EARLY + LATE) * NI + 2 * m
         tiles[p, row:row + 1] = exports[m][0:1]
         tiles[p, row + 1:row + 2] = exports[m][NI - 1:]
-    cast(1)
     out_rows = zero
     for row, x in ((0, exports[0][0:1]), (1, exports[1][0:1]), (NI - 2, exports[1][NI - 1:]), (NI - 1, exports[0][NI - 1:])):
         out_rows = jnp.where(sub == row, jnp.broadcast_to(x, (NI, NJ)), out_rows)
-    pack_strips(1, -1.0, totals[0], totals[1], out_rows)
+    ns_rows = []
+    for m, x in enumerate(exports_ns):
+        x = -FRICTION * x
+        x = jnp.where(lane == 0, pltpu.roll(x, 1, 1), jnp.where(lane == NJ - 1, pltpu.roll(x, NJ - 1, 1), 0.0))
+        x = jnp.sum(pltpu.roll(x, 0, 1, stride=width, stride_axis=0), axis=0, keepdims=True)
+        row = (EARLY + LATE) * NI + 4 + m
+        tiles[p, row:row + 1] = x
+        ns_rows.append(jnp.broadcast_to(x, (NI, NJ)))
+    pack_strips(1, -1.0, (*totals, out_rows), ns_rows)
     cast_strips(1)
-    rest = pl.ds(REST, 4 * K)
-    copy(pack_out.at[0, rest], pack_in.at[1, rest], east_dev, q, send_sem.at[0], chunk_sem.at[NC + 1]).start()
-    copy(pack_out.at[1, rest], pack_in.at[0, rest], west_dev, q, send_sem.at[0], chunk_sem.at[NC + 1]).start()
+    cast(1)
+
+    for side, d in enumerate((NI - 1, 0)):
+        for m in range(2):
+            row = REST + (2 + m) * K
+            pack_out[side, row:row + K, :] = laps[m, :, d, :]
+    n2 = s2 = zero
+    for m in range(2):
+        for k in range(K):
+            n2 = put(n2, laps[m, k], NJ - 1, m * K + k)
+            s2 = put(s2, laps[m, k], 0, m * K + k)
+    lap_edges[0] = n2
+    lap_edges[1] = s2
 
     cast_wait(0)
     flat = tiles.reshape(n_lon * TILES * NI, NJ)
@@ -530,8 +488,10 @@
             outer.append(jnp.where(lanes < width, pltpu.roll(north, (NJ - width * s) % NJ, 1), x))
         return [main, outer]
 
-    def late_wait():
-        cast_wait(1)
+    def rim_rows(f):
+        north = flat_rim[pl.ds(f, n_lon, stride=NI), :]
+        south = jnp.where(not_south, flat_rim[pl.ds(n_lon * NI + f, n_lon, stride=NI), :], 0.0)
+        return jnp.where(lanes % width == width - 1, north, south)
 
     def share(total):
         sums[q] = jnp.broadcast_to(total, (NI, NJ))
@@ -539,7 +499,14 @@
             lat = lax.rem(q + r, n_lat)
             copy(sums.at[q], sums.at[q], p, lat, cast_send.at[3], cast_recv.at[2, 0]).start()
 
-    x, slope_x, slope_y = surface_solve(loader, late_wait, share, n_lon, K, NI, NJ)
+    rest = pl.ds(REST, 4 * K)
+
+    def late_wait():
+        meet(lap_edges, lap_slots, 2)
+        sides(REST, 4 * K, NC)
+        cast_wait(1)
+
+    x, slope_x, slope_y = surface_solve(loader, rim_rows, late_wait, share, n_lon, K, NI, NJ)
     for i, field in enumerate((x, slope_x, slope_y)):
         for s in range(NI):
             held[i, pl.ds(s, n_lon, stride=NI), :] = field[s]
@@ -547,46 +514,10 @@
     ox_ref[0] = held[0, block, :]
     slope_u = GRAVITY * held[1, block, :]
     slope_v = GRAVITY * held[2, block, :]
-    drain(pack_in.at[:, rest], chunk_sem.at[NC + 1])
-    turned = zero
-    for i, row in enumerate((pne0[0:1], pse0[0:1], pnw0[NI - 1:], psw0[NI - 1:])):
-        turned = jnp.where(sub == i, jnp.broadcast_to(row, (NI, NJ)), turned)
-    turned = flip_lanes(turned)
-    after = pltpu.roll(turned, 1, 1)
-    corners = ((wide(turned[0:1]), wide(after[1:2])), (wide(turned[2:3]), wide(after[3:4])))
-    corner_depths = ((pne1[0:1], pse1[0:1]), (pnw1[NI - 1:], psw1[NI - 1:]))
-    side_depths = []
-    for side, d1 in enumerate((NI - 1, 0)):
-        base = pack_in[side, BASE:REST, :]
-        cn1, cs1 = corner_depths[side]
-        d = wide(base[0:1, :])
-        dn = jnp.where(lane_c == NJ - 1, jnp.broadcast_to(cn1[:, 0:1], (KC, NJ)), pltpu.roll(d, NJ - 1, 1))
-        ds = jnp.where(lane_c == 0, jnp.broadcast_to(cs1[:, 0:1], (KC, NJ)), pltpu.roll(d, 1, 1))
-        own = wide(depth[d1:d1 + 1, :])
-        side_depths.append([jnp.minimum(d, o) for o in (wide(base[1:2, :]), own, dn, ds)])
-
-    for c in range(NC):
-        level_c = row_c.astype(F32) + (c * KC + 0.5)
-
-        def part(d, x):
-            return jnp.where(level_c < d, x, 0.0)
-
-        for side in range(2):
-            far, own, dn, ds = side_depths[side]
-            cn0, cs0 = corners[side]
-            for m in range(2):
-                row = c * SIDE + m * KC
-                outer = REST + (2 + m) * K + c * KC
-                x = pack_in[side, row:row + KC, :]
-                at = (2 + m) * K + c * KC
-                cn = pltpu.roll(cn0, at, 1, stride=1, stride_axis=0)
-                cs = pltpu.roll(cs0, at, 1, stride=1, stride_axis=0)
-                xn = jnp.where(lane_c == NJ - 1, cn, pltpu.roll(x, NJ - 1, 1))
-                xs = jnp.where(lane_c == 0, cs, pltpu.roll(x, 1, 1))
-                total = part(far, pack_in[side, outer:outer + KC, :] - x)
-                total = total + part(own, pack_out[side, row:row + KC, :] - x)
-                side_lap[c, 2 * side + m] = total + (part(dn, xn - x) + part(ds, xs - x))
-
+    drain(pack_in.at[:, rest], chunk_sem.at[NC])
+    met(lap_slots, 2)
+    rim[4] = jnp.where(at_pole, -flip_rows(lap_slots[0]), lap_slots[0])
+    rim[5] = jnp.where(not_south, lap_slots[1], 0.0)
     both_e = jnp.minimum(depth, shift_e(depth, base_e))
     both_w = jnp.minimum(depth, shift_w(depth, base_w))
     both_n = jnp.where(lane == NJ - 1, near_ns, near_n)
@@ -601,12 +532,11 @@
     def around(c, inner, ref, f):
         k = c * KC + inner
         x = ref[k]
-        row = pl.ds(c * SIDE + (f - 2) * KC + inner if f >= 2 else REST + f * K + k, 1)
+        row = pl.ds(NI + c * SIDE + (f - 2) * KC + inner if f >= 2 else REST + f * K + k, 1)
         return (x, shift_e(x, pack_in[0, row, :]), shift_w(x, pack_in[1, row, :]),
                 shift_n(x, rim[0], f * K + k), shift_s(x, rim[1], f * K + k))
 
     def tracers(c, i, carry):
-        inner = pl.ds(i, 1)
         k = c * KC + i
         flux_t, flux_s = carry
         kf = lax.convert_element_type(k, F32) + 0.5
@@ -645,8 +575,12 @@
         ot_ref[k] = new_t
         os_ref[k] = new_s
         for m, (out, slope) in enumerate(((ou_ref, slope_u), (ov_ref, slope_v))):
-            lap_ew = jnp.where(is_w, side_lap[c, 2 + m, inner, :], side_lap[c, m, inner, :])
-            star = out[k] - FRICTION * gate(near_ew, kf, lap_ew)
+            row = pl.ds(REST + (2 + m) * K + k, 1)
+            lap_ew = jnp.where(is_w, pack_in[1, row, :], pack_in[0, row, :])
+            at = m * K + k
+            lap_n = pltpu.roll(rim[4], NJ - 1 - at, 1)
+            lap_ns = jnp.where(is_s, pltpu.roll(rim[5], lax.rem(NJ - at, NJ), 1), lap_n)
+            star = out[k] - FRICTION * (gate(near_ew, kf, lap_ew) + gate(near_ns, kf, lap_ns))
             out[k] = gate(depth, kf, star - slope)
         return flux_t, flux_s
 
@@ -659,20 +593,16 @@
 
     drain(pack_out, send_sem.at[0])
 
+    sent = pack_in.at[0, 0:3 * NI]
+
     @pl.when(not_south)
     def _():
-        drain(pack_in.at[0, full], send_sem.at[1])
-
-    @pl.when(both_remote)
-    def _():
-        drain(pack_in.at[0, full], send_sem.at[2])
-
-    @pl.when(one_remote)
-    def _():
-        drain(pack_in.at[0, pl.ds(0, 2 * NI + 2)], send_sem.at[2])
-
-    used = pl.ds(0, TILES)
-    drain(tiles.at[pl.ds(0, n_lon - 1), pl.ds(0, (EARLY + LATE) * NI + 4)], cast_send.at[0])
+        drain(sent, send_sem.at[1])
+
+    drain(sent, send_sem.at[2])
+
+    used = pl.ds(0, NI)
+    drain(tiles.at[pl.ds(0, n_lon - 1), pl.ds(0, (EARLY + LATE) * NI + 6)], cast_send.at[0])
 
     @pl.when(not_south)
     def _():
@@ -692,10 +622,12 @@
     drain(sums.at[pl.ds(0, n_lat - 1)], cast_send.at[3])
 
 
-def surface_solve(load, late_wait, share, n_lon, K, NI, NJ):
+def surface_solve(load, rim_rows, late_wait, share, n_lon, K, NI, NJ):
+    width = NJ // NI
     tiles = range(2)
     lines = range(NI)
     lane = iota((n_lon, NJ), 1)
+    edge = jnp.logical_or(lane == 0, lane == NJ - 1)
 
     def every(fn, *arrays):
         return [[fn(*(a[b][s] for a in arrays)) for s in lines] for b in tiles]
@@ -774,6 +706,11 @@
         for b, (from_w, from_e) in enumerate(((inner[2 * m], inner[2 * m + 1]), (outer[m], outer[NI - 1 - m]))):
             t[b][NI - 1] = t[b][NI - 1] + pltpu.roll(from_w, n_lon - 1, 0)
             t[b][0] = t[b][0] + pltpu.roll(from_e, 1, 0)
+        own, beyond = inner[4 + m], rim_rows(EARLY + LATE + 1 + m)
+        for s in lines:
+            for b, row in ((0, beyond), (1, own)):
+                moved = pltpu.roll(row, (NJ - width * s) % NJ, 1) if s else row
+                t[b][s] = t[b][s] + jnp.where(edge, moved, 0.0)
     residual = every(
         lambda h, d, e, w, n, s: d - jnp.where(h > 0.0, 0.5 * DIVERGENCE * ((e - w) + (n - s)), 0.0),
         height, start, east(t_u), west(t_u), north(t_v), south(t_v))
@@ -819,7 +756,7 @@
     big = jax.ShapeDtypeStruct((K, NI, NJ), F32)
     tile = jax.ShapeDtypeStruct((NI, NJ), F32)
     one = jax.ShapeDtypeStruct((1,), F32)
-    pack = pltpu.VMEM((2, 7 * K + NI, NJ), F32)
+    pack = pltpu.VMEM((2, NI + NC * 3 * KC + 4 * K, NJ), F32)
 
     def room(*lead):
         return pltpu.VMEM((*lead, NI, NJ), F32)
@@ -831,11 +768,11 @@
         out_specs=(vmem,) * 2,
         scratch_shapes=[
             room(4, K), pltpu.VMEM((2, NI, NJ), jnp.int32), room(2), pltpu.SMEM((K,), F32),
-            pack, pack, room(2, 2), room(6, 2), room(6), pltpu.VMEM((NC, 4, KC, NJ), F32),
+            pack, pack, room(2, 2), room(2, 2), room(2), room(2), room(6),
             room(2, K), room(K), pltpu.VMEM((n_lon, TILES * NI, NJ), F32), room(2), room(2, n_lon), room(n_lat),
             pltpu.VMEM((3, n_lon * NI, NJ), F32),
-            pltpu.SemaphoreType.DMA((3,)), pltpu.SemaphoreType.DMA((3,)), pltpu.SemaphoreType.DMA((NC + 2,)),
-            pltpu.SemaphoreType.DMA((2,)), pltpu.SemaphoreType.DMA((4,)), pltpu.SemaphoreType.DMA((3, 3)),
+            pltpu.SemaphoreType.DMA((3,)), pltpu.SemaphoreType.DMA((3,)), pltpu.SemaphoreType.DMA((NC + 1,)),
+            pltpu.SemaphoreType.DMA((4,)), pltpu.SemaphoreType.DMA((4,)), pltpu.SemaphoreType.DMA((3, 3)),
         ],
         compiler_params=pltpu.CompilerParams(
             collective_id=0, has_side_effects=True),

time: 22.6 us -> 22 us (0.973)
  Pallas kernels: 21.8 us -> 21.2 us
    pallas_call x1, Pallas kernels: 20.9 us -> 20.4 us  [per_device(): pl.pallas_call(functools.partial(step_kernel, n_lon, n_lat, KC), out_shap...]
where the time goes in v2:
time: 22 us; the launch traced here: 21.8 us
  Pallas kernels  21.2 us (96%)
  between operations  0.64 us (3%)
    pallas_call x1, Pallas kernels, per_device(): pl.pallas_call(functools.partial(step_kernel, n_lon, n_lat, KC), out_shap...  20.4 us
    pallas_call x1, Pallas kernels, per_device(): pl.pallas_call(finish_kernel, out_shape=(big, big, big, big, tile, one),...  0.82 us

profile of v2, /device:TPU:0, one launch (start us, length us, event | category | flops | bytes accessed | tf_op | source)
XLA Modules:
  0.0 21.8 jit_solution(18085976345934387907)
XLA Ops:
  0.6 20.4 %step.1 = (f32[4,32,8,128]{3,2,1,0:T(8,128)S(1)}, f32[2,8,128]{2,1,0:T(8,128)S(1)}) custom-call(f32[32,8,128]{2,1,0:T(8,128)} %refs_0_.1, f32[32,8,128]{2,1,0:T(8,128)} %refs_1_.1, f32[32,8,128]{2,1,0:T(8,128)} %refs_2_.1, f32[32,8,128]{2,1,0:T(8,128)} %refs_3_.1, s32[8,128]{1,0:T(8,128)} %refs_4_.1, s32[8,128]{1,0:T(8,128)} %refs_5_.1, f32[32]{0:T(128)} %refs_6_.1, ...), custom_call_target="tpu_custom_call" | custom-call | tf_op jit(solution)/shard_map/step/pallas_call | solution.py:764
  21.0 0.8 %finish.1 = (f32[32,8,128]{2,1,0:T(8,128)}, f32[32,8,128]{2,1,0:T(8,128)}, f32[32,8,128]{2,1,0:T(8,128)}, f32[32,8,128]{2,1,0:T(8,128)}, f32[8,128]{1,0:T(8,128)}, /*index=5*/f32[1]{0:T(128)}) custom-call(f32[4,32,8,128]{3,2,1,0:T(8,128)S(1)} %get-tuple-element.14.kept, f32[2,8,128]{2,1,0:T(8,128)S(1)} %get-tuple-element.15.x_ref), custom_call_target="tpu_custom_call" | custom-call | tf_op jit(solution)/shard_map/finish/pallas_call | solution.py:781

commit v3 on v2

--- a/solution.py
+++ b/solution.py
@@ -33,27 +33,16 @@
     return lax.broadcasted_iota(jnp.int32, shape, axis)
 
 
+def flip(x, axis):
+    return jnp.take_along_axis(x, x.shape[axis] - 1 - iota(x.shape, axis), axis=axis)
+
+
 def flip_rows(x):
-    n = x.shape[0]
-    row = iota(x.shape, 0)
-    bit = n // 2
-    while bit:
-        up = pltpu.roll(x, bit, 0)
-        down = pltpu.roll(x, n - bit, 0)
-        x = up if 2 * bit == n else jnp.where((row & bit) != 0, up, down)
-        bit //= 2
-    return x
+    return flip(x, 0)
 
 
 def flip_lanes(x):
-    n = x.shape[1]
-    lane = iota(x.shape, 1)
-    bit = n // 2
-    while bit:
-        up = pltpu.roll(x, bit, 1)
-        x = up if 2 * bit == n else jnp.where((lane & bit) != 0, up, pltpu.roll(x, n - bit, 1))
-        bit //= 2
-    return x
+    return flip(x, 1)
 
 
 def step_kernel(n_lon, n_lat, KC, *refs):
@@ -63,7 +52,7 @@
      rims, sums, held, load_sem, send_sem, chunk_sem, edge_sem, cast_send, cast_recv) = refs
     _, K, NI, NJ = fields.shape
     NC = K // KC
-    SIDE = 3 * KC
+    SIDE = 2 * KC
     REST = NI + NC * SIDE
     t_ref, s_ref, u_ref, v_ref = (fields.at[f] for f in range(4))
     ot_ref, os_ref, ou_ref, ov_ref = (kept.at[f] for f in range(4))
@@ -141,39 +130,15 @@
     lane = iota((NI, NJ), 1)
     depth = (num_ref[...] * sea_ref[...]).astype(F32)
 
-    row_c = iota((KC, NJ), 0)
-    lane_c = iota((KC, NJ), 1)
-    thick_c = []
-    for c in range(NC):
-        h = jnp.zeros((KC, NJ), F32)
-        for i in range(KC):
-            h = jnp.where(row_c == i, thick_ref[c * KC + i], h)
-        thick_c.append(h)
-
-    def wide(row):
-        return jnp.broadcast_to(row, (KC, NJ))
-
     for side, d1 in enumerate((NI - 1, 0)):
-        own_depth = wide(depth[d1:d1 + 1, :])
-        carried = jnp.zeros((KC, NJ), F32)
         for c in range(NC):
             levels = slice(c * KC, (c + 1) * KC)
-            row = NI + c * SIDE
-            pack_out[side, row:row + KC, :] = u_ref[levels, d1, :]
-            pack_out[side, row + KC:row + 2 * KC, :] = v_ref[levels, d1, :]
-            t_col, s_col = t_ref[levels, d1, :], s_ref[levels, d1, :]
-            wet = own_depth > row_c.astype(F32) + (c * KC + 0.5)
-            x = jnp.where(wet, (CONTRACTION * s_col - EXPANSION * t_col) * thick_c[c], 0.0)
-            step = 1
-            while step < KC:
-                x = x + jnp.where(row_c >= step, pltpu.roll(x, step, 0), 0.0)
-                step *= 2
-            x = x + carried
-            pack_out[side, row + 2 * KC:row + 3 * KC, :] = x
-            carried = wide(x[KC - 1:KC, :])
-            for f, x in enumerate((t_col, s_col)):
-                row = REST + f * K + c * KC
-                pack_out[side, row:row + KC, :] = x
+            for m, ref in enumerate((u_ref, v_ref)):
+                row = NI + c * SIDE + m * KC
+                pack_out[side, row:row + KC, :] = ref[levels, d1, :]
+        for m, ref in enumerate((t_ref, s_ref)):
+            row = REST + m * K
+            pack_out[side, row:row + K, :] = ref[:, d1, :]
         pack_out[side, 0:NI, :] = jnp.broadcast_to(depth[d1:d1 + 1, :], (NI, NJ))
 
     zero = jnp.zeros((NI, NJ), F32)
@@ -283,13 +248,15 @@
         def _():
             around_lon(0, n_lon, lambda lon: send(0, 0, p, lon, q - 1, 1))
 
+        pole = at_pole.astype(jnp.int32)
+        side, lat = 1 - pole, q + 1 - pole
+        slot = jnp.where(at_pole, mirror, p)
+
         @pl.when(not_pole)
         def _():
-            around_lon(0, n_lon, lambda lon: send(1, 1, p, lon, q + 1, 2))
-
-        @pl.when(at_pole)
-        def _():
-            around_lon(1, n_lon, lambda lon: send(1, 0, mirror, lon, q, 2))
+            around_lon(0, 1, lambda lon: send(1, 1, p, lon, q + 1, 2))
+
+        around_lon(1, n_lon, lambda lon: send(1, side, slot, lon, lat, 2))
 
     def cast_wait(which):
         first, count, size = parts[which]
@@ -312,13 +279,6 @@
     for i, x in enumerate((height, first_guess, drive_ref[...])):
         tiles[p, i * NI:(i + 1) * NI] = x
     pack_strips(0, 1.0, (height, first_guess, drive_ref[...]))
-    cast(0)
-    cast_strips(0)
-    level_i = lane - K * (lane // K)
-    level_l = level_i.astype(F32) + 0.5
-    thick_l = zero
-    for k in range(K):
-        thick_l = jnp.where(level_i == k, thick_ref[k], thick_l)
 
     near_e = jnp.where(sub == NI - 1, 0.0, jnp.minimum(depth, pltpu.roll(depth, NI - 1, 0)))
     near_w = jnp.where(sub == 0, 0.0, jnp.minimum(depth, pltpu.roll(depth, 1, 0)))
@@ -354,6 +314,9 @@
 
     lax.fori_loop(0, NC, before_chunk, zero)
 
+    cast(0)
+    cast_strips(0)
+    sides(REST, 2 * K, NC)
     met(slots, 0)
 
     sign = jnp.where(lane >= 2 * K, -1.0, 1.0).astype(F32)
@@ -371,24 +334,8 @@
     def shift_w(x, row):
         return jnp.where(sub == 0, row, pltpu.roll(x, 1, 0))
 
-    def wet_l(d):
-        return jnp.where(level_l < d, 1.0, 0.0)
-
-    def spread(x, i):
-        return jnp.broadcast_to(x[:, i:i + 1], (NI, NJ))
-
-    def packed_pressure(c0, c1):
-        x = (CONTRACTION * pltpu.roll(c0, NJ - K, 1) - EXPANSION * c0) * thick_l * wet_l(spread(c1, 0))
-        step = 1
-        while step < K:
-            x = x + jnp.where(level_i >= step, pltpu.roll(x, step, 1), 0.0)
-            step *= 2
-        return x
-
     rim[0] = pn0
     rim[1] = ps0
-    rim[2] = packed_pressure(pn0, pn1)
-    rim[3] = packed_pressure(ps0, ps1)
 
     drain(pack_in.at[:, 0:starts[1]], chunk_sem.at[0])
     base_e = pack_in[0, 0:1, :]
@@ -423,25 +370,27 @@
             kf = k + 0.5
             h = thick_ref[k]
             pc = pressure[k]
-            u_part = ou_ref[k] + scale_ew * gate(near_ew, kf, side_ew(c, 2 * KC + i) - pc)
-            v_part = ov_ref[k] + scale_ns * gate(near_ns, kf, rim_ns(rim[2], rim[3], k) - pc)
+            push_ew = scale_ew * gate(near_ew, kf, pc)
+            push_ns = scale_ns * gate(near_ns, kf, pc)
+            exports[0] = exports[0] - h * push_ew
+            exports_ns[1] = exports_ns[1] - h * push_ns
+            u_part = ou_ref[k] - push_ew
+            v_part = ov_ref[k] - push_ns
             for m, (x, part, out) in enumerate(((u_ref[k], u_part, ou_ref), (v_ref[k], v_part, ov_ref))):
                 at = (2 + m) * K + k
                 lap = laps[m, k] + gate(near_ew, kf, side_ew(c, m * KC + i) - x)
                 lap = lap + gate(near_ns, kf, rim_ns(rim[0], rim[1], at) - x)
-                edge_lap = gate(near_ew, kf, lap)
+                edge_lap = FRICTION * gate(near_ew, kf, lap)
                 laps[m, k] = lap
-                edge_ns = gate(near_ns, kf, lap)
-                friction = inner_lap(lap, kf) - edge_lap - edge_ns
-                star = gate(depth, kf, part - FRICTION * friction)
+                edge_ns = FRICTION * gate(near_ns, kf, lap)
+                star = gate(depth, kf, part - FRICTION * inner_lap(lap, kf) + (edge_lap + edge_ns))
                 out[k] = star
                 totals[m] = totals[m] + h * star
-                exports[m] = exports[m] + h * edge_lap
-                exports_ns[m] = exports_ns[m] + h * edge_ns
+                exports[m] = exports[m] - h * edge_lap
+                exports_ns[m] = exports_ns[m] - h * edge_ns
 
     tiles[p, EARLY * NI:(EARLY + 1) * NI] = totals[0]
     tiles[p, (EARLY + 1) * NI:(EARLY + 2) * NI] = totals[1]
-    exports = [-FRICTION * x for x in exports]
     for m in range(2):
         row = (EARLY + LATE) * NI + 2 * m
         tiles[p, row:row + 1] = exports[m][0:1]
@@ -451,27 +400,29 @@
         out_rows = jnp.where(sub == row, jnp.broadcast_to(x, (NI, NJ)), out_rows)
     ns_rows = []
     for m, x in enumerate(exports_ns):
-        x = -FRICTION * x
         x = jnp.where(lane == 0, pltpu.roll(x, 1, 1), jnp.where(lane == NJ - 1, pltpu.roll(x, NJ - 1, 1), 0.0))
         x = jnp.sum(pltpu.roll(x, 0, 1, stride=width, stride_axis=0), axis=0, keepdims=True)
         row = (EARLY + LATE) * NI + 4 + m
         tiles[p, row:row + 1] = x
         ns_rows.append(jnp.broadcast_to(x, (NI, NJ)))
     pack_strips(1, -1.0, (*totals, out_rows), ns_rows)
+    cast(1)
     cast_strips(1)
-    cast(1)
-
+
+    levels_out = (pressure, laps.at[0], laps.at[1])
     for side, d in enumerate((NI - 1, 0)):
-        for m in range(2):
+        for m, x in enumerate(levels_out):
             row = REST + (2 + m) * K
-            pack_out[side, row:row + K, :] = laps[m, :, d, :]
+            pack_out[side, row:row + K, :] = x[:, d, :]
     n2 = s2 = zero
-    for m in range(2):
+    for m, x in enumerate(levels_out):
         for k in range(K):
-            n2 = put(n2, laps[m, k], NJ - 1, m * K + k)
-            s2 = put(s2, laps[m, k], 0, m * K + k)
+            n2 = put(n2, x[k], NJ - 1, m * K + k)
+            s2 = put(s2, x[k], 0, m * K + k)
     lap_edges[0] = n2
     lap_edges[1] = s2
+    meet(lap_edges, lap_slots, 2)
+    sides(REST + 2 * K, 3 * K, NC + 1)
 
     cast_wait(0)
     flat = tiles.reshape(n_lon * TILES * NI, NJ)
@@ -499,11 +450,8 @@
             lat = lax.rem(q + r, n_lat)
             copy(sums.at[q], sums.at[q], p, lat, cast_send.at[3], cast_recv.at[2, 0]).start()
 
-    rest = pl.ds(REST, 4 * K)
 
     def late_wait():
-        meet(lap_edges, lap_slots, 2)
-        sides(REST, 4 * K, NC)
         cast_wait(1)
 
     x, slope_x, slope_y = surface_solve(loader, rim_rows, late_wait, share, n_lon, K, NI, NJ)
@@ -514,10 +462,12 @@
     ox_ref[0] = held[0, block, :]
     slope_u = GRAVITY * held[1, block, :]
     slope_v = GRAVITY * held[2, block, :]
-    drain(pack_in.at[:, rest], chunk_sem.at[NC])
+    drain(pack_in.at[:, REST:REST + 2 * K], chunk_sem.at[NC])
+    drain(pack_in.at[:, REST + 2 * K:], chunk_sem.at[NC + 1])
     met(lap_slots, 2)
-    rim[4] = jnp.where(at_pole, -flip_rows(lap_slots[0]), lap_slots[0])
-    rim[5] = jnp.where(not_south, lap_slots[1], 0.0)
+    fold = jnp.where(lane < K, 1.0, -1.0)
+    rim[2] = jnp.where(at_pole, flip_rows(lap_slots[0]) * fold, lap_slots[0])
+    rim[3] = jnp.where(not_south, lap_slots[1], 0.0)
     both_e = jnp.minimum(depth, shift_e(depth, base_e))
     both_w = jnp.minimum(depth, shift_w(depth, base_w))
     both_n = jnp.where(lane == NJ - 1, near_ns, near_n)
@@ -535,6 +485,15 @@
         row = pl.ds(NI + c * SIDE + (f - 2) * KC + inner if f >= 2 else REST + f * K + k, 1)
         return (x, shift_e(x, pack_in[0, row, :]), shift_w(x, pack_in[1, row, :]),
                 shift_n(x, rim[0], f * K + k), shift_s(x, rim[1], f * K + k))
+
+    def beyond_ew(f, k):
+        row = pl.ds(REST + f * K + k, 1)
+        return jnp.where(is_w, pack_in[1, row, :], pack_in[0, row, :])
+
+    def beyond_ns(f, k):
+        at = f * K + k
+        north = pltpu.roll(rim[2], NJ - 1 - at, 1)
+        return jnp.where(is_s, pltpu.roll(rim[3], lax.rem(NJ - at, NJ), 1), north)
 
     def tracers(c, i, carry):
         k = c * KC + i
@@ -575,12 +534,13 @@
         ot_ref[k] = new_t
         os_ref[k] = new_s
         for m, (out, slope) in enumerate(((ou_ref, slope_u), (ov_ref, slope_v))):
-            row = pl.ds(REST + (2 + m) * K + k, 1)
-            lap_ew = jnp.where(is_w, pack_in[1, row, :], pack_in[0, row, :])
-            at = m * K + k
-            lap_n = pltpu.roll(rim[4], NJ - 1 - at, 1)
-            lap_ns = jnp.where(is_s, pltpu.roll(rim[5], lax.rem(NJ - at, NJ), 1), lap_n)
-            star = out[k] - FRICTION * (gate(near_ew, kf, lap_ew) + gate(near_ns, kf, lap_ns))
+            lap_ew, lap_ns = beyond_ew(3 + m, k), beyond_ns(1 + m, k)
+            push = -FRICTION * (gate(near_ew, kf, lap_ew) + gate(near_ns, kf, lap_ns))
+            if m == 0:
+                push = push + scale_ew * gate(near_ew, kf, beyond_ew(2, k))
+            else:
+                push = push + scale_ns * gate(near_ns, kf, beyond_ns(0, k))
+            star = out[k] + push
             out[k] = gate(depth, kf, star - slope)
         return flux_t, flux_s
 
@@ -756,7 +716,7 @@
     big = jax.ShapeDtypeStruct((K, NI, NJ), F32)
     tile = jax.ShapeDtypeStruct((NI, NJ), F32)
     one = jax.ShapeDtypeStruct((1,), F32)
-    pack = pltpu.VMEM((2, NI + NC * 3 * KC + 4 * K, NJ), F32)
+    pack = pltpu.VMEM((2, NI + NC * 2 * KC + 5 * K, NJ), F32)
 
     def room(*lead):
         return pltpu.VMEM((*lead, NI, NJ), F32)
@@ -768,10 +728,10 @@
         out_specs=(vmem,) * 2,
         scratch_shapes=[
             room(4, K), pltpu.VMEM((2, NI, NJ), jnp.int32), room(2), pltpu.SMEM((K,), F32),
-            pack, pack, room(2, 2), room(2, 2), room(2), room(2), room(6),
+            pack, pack, room(2, 2), room(2, 2), room(2), room(2), room(4),
             room(2, K), room(K), pltpu.VMEM((n_lon, TILES * NI, NJ), F32), room(2), room(2, n_lon), room(n_lat),
             pltpu.VMEM((3, n_lon * NI, NJ), F32),
-            pltpu.SemaphoreType.DMA((3,)), pltpu.SemaphoreType.DMA((3,)), pltpu.SemaphoreType.DMA((NC + 1,)),
+            pltpu.SemaphoreType.DMA((3,)), pltpu.SemaphoreType.DMA((3,)), pltpu.SemaphoreType.DMA((NC + 2,)),
             pltpu.SemaphoreType.DMA((4,)), pltpu.SemaphoreType.DMA((4,)), pltpu.SemaphoreType.DMA((3, 3)),
         ],
         compiler_params=pltpu.CompilerParams(

time: 22 us -> 21.7 us (0.986)
  Pallas kernels: 21.2 us -> 20.9 us
    pallas_call x1, Pallas kernels: 20.4 us -> 20.1 us  [per_device(): pl.pallas_call(functools.partial(step_kernel, n_lon, n_lat, KC), out_shap...]
where the time goes in v3:
time: 21.7 us; the launch traced here: 21.6 us
  Pallas kernels  20.9 us (96%)
  between operations  0.64 us (3%)
    pallas_call x1, Pallas kernels, per_device(): pl.pallas_call(functools.partial(step_kernel, n_lon, n_lat, KC), out_shap...  20.1 us
    pallas_call x1, Pallas kernels, per_device(): pl.pallas_call(finish_kernel, out_shape=(big, big, big, big, tile, one),...  0.82 us

profile of v3, /device:TPU:0, one launch (start us, length us, event | category | flops | bytes accessed | tf_op | source)
XLA Modules:
  0.0 21.6 jit_solution(7092390511517881860)
XLA Ops:
  0.6 20.1 %step.1 = (f32[4,32,8,128]{3,2,1,0:T(8,128)S(1)}, f32[2,8,128]{2,1,0:T(8,128)S(1)}) custom-call(f32[32,8,128]{2,1,0:T(8,128)} %refs_0_.1, f32[32,8,128]{2,1,0:T(8,128)} %refs_1_.1, f32[32,8,128]{2,1,0:T(8,128)} %refs_2_.1, f32[32,8,128]{2,1,0:T(8,128)} %refs_3_.1, s32[8,128]{1,0:T(8,128)} %refs_4_.1, s32[8,128]{1,0:T(8,128)} %refs_5_.1, f32[32]{0:T(128)} %refs_6_.1, ...), custom_call_target="tpu_custom_call" | custom-call | tf_op jit(solution)/shard_map/step/pallas_call | solution.py:724
  20.7 0.8 %finish.1 = (f32[32,8,128]{2,1,0:T(8,128)}, f32[32,8,128]{2,1,0:T(8,128)}, f32[32,8,128]{2,1,0:T(8,128)}, f32[32,8,128]{2,1,0:T(8,128)}, f32[8,128]{1,0:T(8,128)}, /*index=5*/f32[1]{0:T(128)}) custom-call(f32[4,32,8,128]{3,2,1,0:T(8,128)S(1)} %get-tuple-element.14.kept, f32[2,8,128]{2,1,0:T(8,128)S(1)} %get-tuple-element.15.x_ref), custom_call_target="tpu_custom_call" | custom-call | tf_op jit(solution)/shard_map/finish/pallas_call | solution.py:741

commit v4 on v3

--- a/solution.py
+++ b/solution.py
@@ -190,8 +190,8 @@
 
     def sides(first, rows, sem):
         rows = pl.ds(first, rows)
+        copy(pack_out.at[1, rows], pack_in.at[0, rows], west_dev, q, send_sem.at[0], chunk_sem.at[sem]).start()
         copy(pack_out.at[0, rows], pack_in.at[1, rows], east_dev, q, send_sem.at[0], chunk_sem.at[sem]).start()
-        copy(pack_out.at[1, rows], pack_in.at[0, rows], west_dev, q, send_sem.at[0], chunk_sem.at[sem]).start()
 
     starts = [0] + [NI + c * SIDE for c in range(1, NC + 1)]
     for c in range(NC):
@@ -231,32 +231,46 @@
         def _():
             rims[0, mirror, rows] = north[:count]
 
+    def each_other(fn):
+        def visit(r, carry):
+            fn(jnp.where(r <= p, r - 1, r))
+            return carry
+
+        if n_lon <= 8:
+            for r in range(1, n_lon):
+                visit(r, 0)
+        else:
+            lax.fori_loop(1, n_lon, visit, 0)
+
     def cast(which):
-        first, _, size = parts[which]
+        first, count, size = parts[which]
         mine = tiles.at[p, pl.ds(first * NI, size)]
-        around_lon(1, n_lon, lambda lon: copy(mine, mine, lon, q, cast_send.at[0], cast_recv.at[which, 0]).start())
-
-    def cast_strips(which):
-        first, count, _ = parts[which]
         rows = pl.ds(first, count)
+        pole = at_pole.astype(jnp.int32)
+        side, lat = 1 - pole, q + 1 - pole
+        slot = jnp.where(at_pole, mirror, p)
 
         def send(way, side, slot, lon, lat, out):
             copy(strips.at[way, rows], rims.at[side, slot, rows], lon, lat, cast_send.at[out],
                  cast_recv.at[which, 1 + side]).start()
 
+        @pl.when(not_pole)
+        def _():
+            send(1, 1, p, p, q + 1, 2)
+
         @pl.when(not_south)
         def _():
-            around_lon(0, n_lon, lambda lon: send(0, 0, p, lon, q - 1, 1))
-
-        pole = at_pole.astype(jnp.int32)
-        side, lat = 1 - pole, q + 1 - pole
-        slot = jnp.where(at_pole, mirror, p)
-
-        @pl.when(not_pole)
-        def _():
-            around_lon(0, 1, lambda lon: send(1, 1, p, lon, q + 1, 2))
-
-        around_lon(1, n_lon, lambda lon: send(1, side, slot, lon, lat, 2))
+            send(0, 0, p, p, q - 1, 1)
+
+        def to(lon):
+            @pl.when(not_south)
+            def _():
+                send(0, 0, p, lon, q - 1, 1)
+
+            send(1, side, slot, lon, lat, 2)
+            copy(mine, mine, lon, q, cast_send.at[0], cast_recv.at[which, 0]).start()
+
+        each_other(to)
 
     def cast_wait(which):
         first, count, size = parts[which]
@@ -315,7 +329,6 @@
     lax.fori_loop(0, NC, before_chunk, zero)
 
     cast(0)
-    cast_strips(0)
     sides(REST, 2 * K, NC)
     met(slots, 0)
 
@@ -407,7 +420,6 @@
         ns_rows.append(jnp.broadcast_to(x, (NI, NJ)))
     pack_strips(1, -1.0, (*totals, out_rows), ns_rows)
     cast(1)
-    cast_strips(1)
 
     levels_out = (pressure, laps.at[0], laps.at[1])
     for side, d in enumerate((NI - 1, 0)):

time: 21.7 us -> 21.1 us (0.972)
  Pallas kernels: 20.9 us -> 20.3 us
    pallas_call x1, Pallas kernels: 20.1 us -> 19.5 us  [per_device(): pl.pallas_call(functools.partial(step_kernel, n_lon, n_lat, KC), out_shap...]
where the time goes in v4:
time: 21.1 us; the launch traced here: 21 us
  Pallas kernels  20.3 us (96%)
  between operations  0.64 us (3%)
    pallas_call x1, Pallas kernels, per_device(): pl.pallas_call(functools.partial(step_kernel, n_lon, n_lat, KC), out_shap...  19.5 us
    pallas_call x1, Pallas kernels, per_device(): pl.pallas_call(finish_kernel, out_shape=(big, big, big, big, tile, one),...  0.82 us

profile of v4, /device:TPU:0, one launch (start us, length us, event | category | flops | bytes accessed | tf_op | source)
XLA Modules:
  0.0 21.0 jit_solution(8605913717593847894)
XLA Ops:
  0.6 19.5 %step.1 = (f32[4,32,8,128]{3,2,1,0:T(8,128)S(1)}, f32[2,8,128]{2,1,0:T(8,128)S(1)}) custom-call(f32[32,8,128]{2,1,0:T(8,128)} %refs_0_.1, f32[32,8,128]{2,1,0:T(8,128)} %refs_1_.1, f32[32,8,128]{2,1,0:T(8,128)} %refs_2_.1, f32[32,8,128]{2,1,0:T(8,128)} %refs_3_.1, s32[8,128]{1,0:T(8,128)} %refs_4_.1, s32[8,128]{1,0:T(8,128)} %refs_5_.1, f32[32]{0:T(128)} %refs_6_.1, ...), custom_call_target="tpu_custom_call" | custom-call | tf_op jit(solution)/shard_map/step/pallas_call | solution.py:736
  20.1 0.8 %finish.1 = (f32[32,8,128]{2,1,0:T(8,128)}, f32[32,8,128]{2,1,0:T(8,128)}, f32[32,8,128]{2,1,0:T(8,128)}, f32[32,8,128]{2,1,0:T(8,128)}, f32[8,128]{1,0:T(8,128)}, /*index=5*/f32[1]{0:T(128)}) custom-call(f32[4,32,8,128]{3,2,1,0:T(8,128)S(1)} %get-tuple-element.14.kept, f32[2,8,128]{2,1,0:T(8,128)S(1)} %get-tuple-element.15.x_ref), custom_call_target="tpu_custom_call" | custom-call | tf_op jit(solution)/shard_map/finish/pallas_call | solution.py:753

commit v5 on v4

--- a/solution.py
+++ b/solution.py
@@ -308,7 +308,8 @@
         total = gate(near_e, kf, pltpu.roll(x, NI - 1, 0) - x) + gate(near_w, kf, pltpu.roll(x, 1, 0) - x)
         return total + (gate(near_n, kf, pltpu.roll(x, NJ - 1, 1) - x) + gate(near_s, kf, pltpu.roll(x, 1, 1) - x))
 
-    def before_level(k, pc):
+    def before_level(k, carry):
+        pc, tu, tv = carry
         kf = lax.convert_element_type(k, F32) + 0.5
         u, v = u_ref[k], v_ref[k]
         laps[0, k] = inner_lap(u, kf)
@@ -317,19 +318,21 @@
         pressure[k] = pc
         grad_x = gate(near_e, kf, pltpu.roll(pc, NI - 1, 0) - pc) + gate(near_w, kf, pc - pltpu.roll(pc, 1, 0))
         grad_y = gate(near_n, kf, pltpu.roll(pc, NJ - 1, 1) - pc) + gate(near_s, kf, pc - pltpu.roll(pc, 1, 1))
-        ou_ref[k] = u + coriolis * v - (0.5 * PRESSURE_SCALE) * grad_x
-        ov_ref[k] = v - coriolis * u - (0.5 * PRESSURE_SCALE) * grad_y
-        return pc
-
-    def before_chunk(c, pc):
+        u_part = u + coriolis * v - (0.5 * PRESSURE_SCALE) * grad_x
+        v_part = v - coriolis * u - (0.5 * PRESSURE_SCALE) * grad_y
+        ou_ref[k] = u_part
+        ov_ref[k] = v_part
+        h = thick_ref[k]
+        return pc, tu + gate(depth, kf, h * u_part), tv + gate(depth, kf, h * v_part)
+
+    def before_chunk(c, carry):
         for i in range(KC):
-            pc = before_level(c * KC + i, pc)
-        return pc
-
-    lax.fori_loop(0, NC, before_chunk, zero)
+            carry = before_level(c * KC + i, carry)
+        return carry
+
+    totals = list(lax.fori_loop(0, NC, before_chunk, (zero,) * 3)[1:])
 
     cast(0)
-    sides(REST, 2 * K, NC)
     met(slots, 0)
 
     sign = jnp.where(lane >= 2 * K, -1.0, 1.0).astype(F32)
@@ -351,6 +354,7 @@
     rim[1] = ps0
 
     drain(pack_in.at[:, 0:starts[1]], chunk_sem.at[0])
+    sides(REST, 2 * K, NC)
     base_e = pack_in[0, 0:1, :]
     base_w = pack_in[1, 0:1, :]
     is_w = sub == 0
@@ -372,9 +376,13 @@
         row = NI + c * SIDE + row
         return jnp.where(is_w, pack_in[1, row:row + 1, :], pack_in[0, row:row + 1, :])
 
-    totals = [zero] * 2
-    exports = [zero] * 2
-    exports_ns = [zero] * 2
+    both_e = jnp.where(sub == NI - 1, near_ew, near_e)
+    both_w = jnp.where(is_w, near_ew, near_w)
+    both_n = jnp.where(lane == NJ - 1, near_ns, near_n)
+    both_s = jnp.where(is_s, near_ns, near_s)
+    overlaps = (both_e, both_w, both_n, both_s)
+    sums_lap = [[zero] * 4 for _ in range(2)]
+    push_ew = push_ns = zero
     for c in range(NC):
         if c:
             drain(pack_in.at[:, starts[c]:starts[c + 1]], chunk_sem.at[c])
@@ -382,25 +390,28 @@
             k = c * KC + i
             kf = k + 0.5
             h = thick_ref[k]
-            pc = pressure[k]
-            push_ew = scale_ew * gate(near_ew, kf, pc)
-            push_ns = scale_ns * gate(near_ns, kf, pc)
-            exports[0] = exports[0] - h * push_ew
-            exports_ns[1] = exports_ns[1] - h * push_ns
-            u_part = ou_ref[k] - push_ew
-            v_part = ov_ref[k] - push_ns
-            for m, (x, part, out) in enumerate(((u_ref[k], u_part, ou_ref), (v_ref[k], v_part, ov_ref))):
-                at = (2 + m) * K + k
+            hp = h * pressure[k]
+            push_ew = push_ew + gate(near_ew, kf, hp)
+            push_ns = push_ns + gate(near_ns, kf, hp)
+            for m, x in enumerate((u_ref[k], v_ref[k])):
                 lap = laps[m, k] + gate(near_ew, kf, side_ew(c, m * KC + i) - x)
-                lap = lap + gate(near_ns, kf, rim_ns(rim[0], rim[1], at) - x)
-                edge_lap = FRICTION * gate(near_ew, kf, lap)
+                lap = lap + gate(near_ns, kf, rim_ns(rim[0], rim[1], (2 + m) * K + k) - x)
                 laps[m, k] = lap
-                edge_ns = FRICTION * gate(near_ns, kf, lap)
-                star = gate(depth, kf, part - FRICTION * inner_lap(lap, kf) + (edge_lap + edge_ns))
-                out[k] = star
-                totals[m] = totals[m] + h * star
-                exports[m] = exports[m] - h * edge_lap
-                exports_ns[m] = exports_ns[m] - h * edge_ns
+                hl = h * lap
+                sums_lap[m] = [a + gate(d, kf, hl) for a, d in zip(sums_lap[m], overlaps)]
+    push_ew = scale_ew * push_ew
+    push_ns = scale_ns * push_ns
+    exports, exports_ns = [], []
+    for m, (a_e, a_w, a_n, a_s) in enumerate(sums_lap):
+        given = jnp.where(sub == NI - 1, 0.0, pltpu.roll(a_w, NI - 1, 0)) + jnp.where(is_w, 0.0, pltpu.roll(a_e, 1, 0))
+        given = given + jnp.where(lane == NJ - 1, 0.0, pltpu.roll(a_s, NJ - 1, 1))
+        given = given + jnp.where(is_s, 0.0, pltpu.roll(a_n, 1, 1))
+        totals[m] = totals[m] + FRICTION * ((a_e + a_w) + (a_n + a_s) - given)
+        exports.append(-FRICTION * jnp.where(is_w, a_w, a_e))
+        exports_ns.append(-FRICTION * jnp.where(is_s, a_s, a_n))
+    totals = [totals[0] - push_ew, totals[1] - push_ns]
+    exports[0] = exports[0] - push_ew
+    exports_ns[1] = exports_ns[1] - push_ns
 
     tiles[p, EARLY * NI:(EARLY + 1) * NI] = totals[0]
     tiles[p, (EARLY + 1) * NI:(EARLY + 2) * NI] = totals[1]
@@ -421,20 +432,33 @@
     pack_strips(1, -1.0, (*totals, out_rows), ns_rows)
     cast(1)
 
-    levels_out = (pressure, laps.at[0], laps.at[1])
-    for side, d in enumerate((NI - 1, 0)):
-        for m, x in enumerate(levels_out):
-            row = REST + (2 + m) * K
-            pack_out[side, row:row + K, :] = x[:, d, :]
+    for side, (d, push) in enumerate(((NI - 1, 0.5 * PRESSURE_SCALE), (0, -0.5 * PRESSURE_SCALE))):
+        row = REST + 2 * K
+        pack_out[side, row:row + K, :] = push * pressure[:, d, :] - FRICTION * laps[0, :, d, :]
+        pack_out[side, row + K:row + 2 * K, :] = -FRICTION * laps[1, :, d, :]
     n2 = s2 = zero
-    for m, x in enumerate(levels_out):
-        for k in range(K):
-            n2 = put(n2, x[k], NJ - 1, m * K + k)
-            s2 = put(s2, x[k], 0, m * K + k)
+    for k in range(K):
+        for m, x in enumerate((-FRICTION * laps[0, k], -FRICTION * laps[1, k] - scale_ns * pressure[k])):
+            n2 = put(n2, x, NJ - 1, m * K + k)
+            s2 = put(s2, x, 0, m * K + k)
     lap_edges[0] = n2
     lap_edges[1] = s2
     meet(lap_edges, lap_slots, 2)
-    sides(REST + 2 * K, 3 * K, NC + 1)
+    sides(REST + 2 * K, 2 * K, NC + 1)
+
+    def level(c, carry):
+        for i in range(KC):
+            k = c * KC + i
+            kf = lax.convert_element_type(k, F32) + 0.5
+            pc = pressure[k]
+            parts = (ou_ref[k] - scale_ew * gate(near_ew, kf, pc), ov_ref[k] - scale_ns * gate(near_ns, kf, pc))
+            for m, (part, out) in enumerate(zip(parts, (ou_ref, ov_ref))):
+                lap = laps[m, k]
+                inner = inner_lap(lap, kf) - gate(near_ew, kf, lap) - gate(near_ns, kf, lap)
+                out[k] = gate(depth, kf, part - FRICTION * inner)
+        return carry
+
+    lax.fori_loop(0, NC, level, 0)
 
     cast_wait(0)
     flat = tiles.reshape(n_lon * TILES * NI, NJ)
@@ -477,14 +501,8 @@
     drain(pack_in.at[:, REST:REST + 2 * K], chunk_sem.at[NC])
     drain(pack_in.at[:, REST + 2 * K:], chunk_sem.at[NC + 1])
     met(lap_slots, 2)
-    fold = jnp.where(lane < K, 1.0, -1.0)
-    rim[2] = jnp.where(at_pole, flip_rows(lap_slots[0]) * fold, lap_slots[0])
+    rim[2] = jnp.where(at_pole, -flip_rows(lap_slots[0]), lap_slots[0])
     rim[3] = jnp.where(not_south, lap_slots[1], 0.0)
-    both_e = jnp.minimum(depth, shift_e(depth, base_e))
-    both_w = jnp.minimum(depth, shift_w(depth, base_w))
-    both_n = jnp.where(lane == NJ - 1, near_ns, near_n)
-    both_s = jnp.where(is_s, near_ns, near_s)
-
     def shift_n(x, packed, source):
         return jnp.where(lane == NJ - 1, pltpu.roll(packed, NJ - 1 - source, 1), pltpu.roll(x, NJ - 1, 1))
 
@@ -546,13 +564,7 @@
         ot_ref[k] = new_t
         os_ref[k] = new_s
         for m, (out, slope) in enumerate(((ou_ref, slope_u), (ov_ref, slope_v))):
-            lap_ew, lap_ns = beyond_ew(3 + m, k), beyond_ns(1 + m, k)
-            push = -FRICTION * (gate(near_ew, kf, lap_ew) + gate(near_ns, kf, lap_ns))
-            if m == 0:
-                push = push + scale_ew * gate(near_ew, kf, beyond_ew(2, k))
-            else:
-                push = push + scale_ns * gate(near_ns, kf, beyond_ns(0, k))
-            star = out[k] + push
+            star = out[k] + gate(near_ew, kf, beyond_ew(2 + m, k)) + gate(near_ns, kf, beyond_ns(m, k))
             out[k] = gate(depth, kf, star - slope)
         return flux_t, flux_s
 
@@ -728,7 +740,7 @@
     big = jax.ShapeDtypeStruct((K, NI, NJ), F32)
     tile = jax.ShapeDtypeStruct((NI, NJ), F32)
     one = jax.ShapeDtypeStruct((1,), F32)
-    pack = pltpu.VMEM((2, NI + NC * 2 * KC + 5 * K, NJ), F32)
+    pack = pltpu.VMEM((2, NI + NC * 2 * KC + 4 * K, NJ), F32)
 
     def room(*lead):
         return pltpu.VMEM((*lead, NI, NJ), F32)

time: 21.1 us -> 20.9 us (level)
    pallas_call x1, Pallas kernels: 19.5 us -> 19.3 us  [per_device(): pl.pallas_call(functools.partial(step_kernel, n_lon, n_lat, KC), out_shap...]
where the time goes in v5:
time: 20.9 us; the launch traced here: 20.8 us
  Pallas kernels  20.1 us (96%)
  between operations  0.64 us (3%)
    pallas_call x1, Pallas kernels, per_device(): pl.pallas_call(functools.partial(step_kernel, n_lon, n_lat, KC), out_shap...  19.3 us
    pallas_call x1, Pallas kernels, per_device(): pl.pallas_call(finish_kernel, out_shape=(big, big, big, big, tile, one),...  0.82 us

profile of v5, /device:TPU:0, one launch (start us, length us, event | category | flops | bytes accessed | tf_op | source)
XLA Modules:
  0.0 20.8 jit_solution(9057832170595423172)
XLA Ops:
  0.6 19.3 %step.1 = (f32[4,32,8,128]{3,2,1,0:T(8,128)S(1)}, f32[2,8,128]{2,1,0:T(8,128)S(1)}) custom-call(f32[32,8,128]{2,1,0:T(8,128)} %refs_0_.1, f32[32,8,128]{2,1,0:T(8,128)} %refs_1_.1, f32[32,8,128]{2,1,0:T(8,128)} %refs_2_.1, f32[32,8,128]{2,1,0:T(8,128)} %refs_3_.1, s32[8,128]{1,0:T(8,128)} %refs_4_.1, s32[8,128]{1,0:T(8,128)} %refs_5_.1, f32[32]{0:T(128)} %refs_6_.1, ...), custom_call_target="tpu_custom_call" | custom-call | tf_op jit(solution)/shard_map/step/pallas_call | solution.py:748
  19.9 0.8 %finish.1 = (f32[32,8,128]{2,1,0:T(8,128)}, f32[32,8,128]{2,1,0:T(8,128)}, f32[32,8,128]{2,1,0:T(8,128)}, f32[32,8,128]{2,1,0:T(8,128)}, f32[8,128]{1,0:T(8,128)}, /*index=5*/f32[1]{0:T(128)}) custom-call(f32[4,32,8,128]{3,2,1,0:T(8,128)S(1)} %get-tuple-element.14.kept, f32[2,8,128]{2,1,0:T(8,128)S(1)} %get-tuple-element.15.x_ref), custom_call_target="tpu_custom_call" | custom-call | tf_op jit(solution)/shard_map/finish/pallas_call | solution.py:765

commit v6 on v5

--- a/solution.py
+++ b/solution.py
@@ -166,11 +166,12 @@
             src_ref=src, dst_ref=dst, send_sem=out, recv_sem=into,
             device_id={"lon": lon, "lat": lat}, device_id_type=MESH)
 
-    def meet(pack, slot, sem):
+    def meet_pole(pack, slot, sem):
         @pl.when(at_pole)
         def _():
             copy(pack.at[0], slot.at[0], mirror, q, send_sem.at[2], edge_sem.at[sem]).start()
 
+    def meet_near(pack, slot, sem):
         @pl.when(not_south)
         def _():
             copy(pack.at[1], slot.at[0], p, q - 1, send_sem.at[1], edge_sem.at[sem]).start()
@@ -186,16 +187,23 @@
         def _():
             drain(slot.at[1], edge_sem.at[sem + 1])
 
-    meet(edges, slots, 0)
+    meet_pole(edges, slots, 0)
+
+    def aside(way, first, rows, sem):
+        rows = pl.ds(first, rows)
+        lon = west_dev if way else east_dev
+        copy(pack_out.at[way, rows], pack_in.at[1 - way, rows], lon, q, send_sem.at[0], chunk_sem.at[sem]).start()
 
     def sides(first, rows, sem):
-        rows = pl.ds(first, rows)
-        copy(pack_out.at[1, rows], pack_in.at[0, rows], west_dev, q, send_sem.at[0], chunk_sem.at[sem]).start()
-        copy(pack_out.at[0, rows], pack_in.at[1, rows], east_dev, q, send_sem.at[0], chunk_sem.at[sem]).start()
-
-    starts = [0] + [NI + c * SIDE for c in range(1, NC + 1)]
-    for c in range(NC):
-        sides(starts[c], starts[c + 1] - starts[c], c)
+        aside(1, first, rows, sem)
+        aside(0, first, rows, sem)
+
+    half = (NC + 1) // 2
+    bounds = ((0, NI + half * SIDE), (NI + half * SIDE, REST)) if NC > 1 else ((0, REST),)
+    for way in (1, 0):
+        for i, (first, last) in enumerate(bounds):
+            aside(way, first, last - first, i)
+    meet_near(edges, slots, 0)
 
     height = zero
     for k in range(K):
@@ -252,7 +260,7 @@
 
         def send(way, side, slot, lon, lat, out):
             copy(strips.at[way, rows], rims.at[side, slot, rows], lon, lat, cast_send.at[out],
-                 cast_recv.at[which, 1 + side]).start()
+                 cast_recv.at[3 * which + 1 + side]).start()
 
         @pl.when(not_pole)
         def _():
@@ -268,26 +276,26 @@
                 send(0, 0, p, lon, q - 1, 1)
 
             send(1, side, slot, lon, lat, 2)
-            copy(mine, mine, lon, q, cast_send.at[0], cast_recv.at[which, 0]).start()
+            copy(mine, mine, lon, q, cast_send.at[0], cast_recv.at[3 * which]).start()
 
         each_other(to)
 
     def cast_wait(which):
         first, count, size = parts[which]
         rows = pl.ds(first, count)
-        drain(tiles.at[pl.ds(0, n_lon - 1), pl.ds(first * NI, size)], cast_recv.at[which, 0])
+        drain(tiles.at[pl.ds(0, n_lon - 1), pl.ds(first * NI, size)], cast_recv.at[3 * which])
 
         @pl.when(at_pole)
         def _():
-            drain(rims.at[0, pl.ds(0, n_lon - 1), rows], cast_recv.at[which, 1])
+            drain(rims.at[0, pl.ds(0, n_lon - 1), rows], cast_recv.at[3 * which + 1])
 
         @pl.when(not_pole)
         def _():
-            drain(rims.at[0, pl.ds(0, n_lon), rows], cast_recv.at[which, 1])
+            drain(rims.at[0, pl.ds(0, n_lon), rows], cast_recv.at[3 * which + 1])
 
         @pl.when(not_south)
         def _():
-            drain(rims.at[1, pl.ds(0, n_lon), rows], cast_recv.at[which, 2])
+            drain(rims.at[1, pl.ds(0, n_lon), rows], cast_recv.at[3 * which + 2])
 
     first_guess = sea_ref[...].astype(F32) * eta_ref[...]
     for i, x in enumerate((height, first_guess, drive_ref[...])):
@@ -353,8 +361,8 @@
     rim[0] = pn0
     rim[1] = ps0
 
-    drain(pack_in.at[:, 0:starts[1]], chunk_sem.at[0])
-    sides(REST, 2 * K, NC)
+    drain(pack_in.at[:, bounds[0][0]:bounds[0][1]], chunk_sem.at[0])
+    sides(REST, 2 * K, 2)
     base_e = pack_in[0, 0:1, :]
     base_w = pack_in[1, 0:1, :]
     is_w = sub == 0
@@ -384,8 +392,8 @@
     sums_lap = [[zero] * 4 for _ in range(2)]
     push_ew = push_ns = zero
     for c in range(NC):
-        if c:
-            drain(pack_in.at[:, starts[c]:starts[c + 1]], chunk_sem.at[c])
+        if c == half and NC > 1:
+            drain(pack_in.at[:, bounds[1][0]:bounds[1][1]], chunk_sem.at[1])
         for i in range(KC):
             k = c * KC + i
             kf = k + 0.5
@@ -443,8 +451,9 @@
             s2 = put(s2, x, 0, m * K + k)
     lap_edges[0] = n2
     lap_edges[1] = s2
-    meet(lap_edges, lap_slots, 2)
-    sides(REST + 2 * K, 2 * K, NC + 1)
+    meet_pole(lap_edges, lap_slots, 2)
+    meet_near(lap_edges, lap_slots, 2)
+    sides(REST + 2 * K, 2 * K, 3)
 
     def level(c, carry):
         for i in range(KC):
@@ -484,7 +493,7 @@
         sums[q] = jnp.broadcast_to(total, (NI, NJ))
         for r in range(1, n_lat):
             lat = lax.rem(q + r, n_lat)
-            copy(sums.at[q], sums.at[q], p, lat, cast_send.at[3], cast_recv.at[2, 0]).start()
+            copy(sums.at[q], sums.at[q], p, lat, cast_send.at[3], cast_recv.at[6]).start()
 
 
     def late_wait():
@@ -498,8 +507,8 @@
     ox_ref[0] = held[0, block, :]
     slope_u = GRAVITY * held[1, block, :]
     slope_v = GRAVITY * held[2, block, :]
-    drain(pack_in.at[:, REST:REST + 2 * K], chunk_sem.at[NC])
-    drain(pack_in.at[:, REST + 2 * K:], chunk_sem.at[NC + 1])
+    drain(pack_in.at[:, REST:REST + 2 * K], chunk_sem.at[2])
+    drain(pack_in.at[:, REST + 2 * K:], chunk_sem.at[3])
     met(lap_slots, 2)
     rim[2] = jnp.where(at_pole, -flip_rows(lap_slots[0]), lap_slots[0])
     rim[3] = jnp.where(not_south, lap_slots[1], 0.0)
@@ -600,7 +609,7 @@
     def _():
         drain(rims.at[0, pl.ds(0, n_lon - 1), used], cast_send.at[2])
 
-    drain(sums.at[pl.ds(0, n_lat - 1)], cast_recv.at[2, 0])
+    drain(sums.at[pl.ds(0, n_lat - 1)], cast_recv.at[6])
     total = functools.reduce(lambda a, b: a + b, [sums[lat] for lat in range(n_lat)])
     ox_ref[1] = jnp.sqrt(total / (n_lon * NI * n_lat * NJ) + EPSILON)
     drain(sums.at[pl.ds(0, n_lat - 1)], cast_send.at[3])
@@ -701,15 +710,30 @@
     mid = 0.5 * (SPECTRUM_HIGH + SPECTRUM_LOW)
     half = 0.5 * (SPECTRUM_HIGH - SPECTRUM_LOW)
     ratio = mid / half
-    direction = every(lambda a: a / mid, precondition(residual))
+
+    def across(d):
+        out = every(lambda wn, n, ws, s: wn * n + ws * s, w_n, north(d), w_s, south(d))
+        for b in tiles:
+            out[b][NI - 1] = out[b][NI - 1] + w_e[b][NI - 1] * pltpu.roll(d[b][0], n_lon - 1, 0)
+            out[b][0] = out[b][0] + w_w[b][0] * pltpu.roll(d[b][NI - 1], 1, 0)
+        return out
+
+    direction = precondition(residual)
+    image = residual
+    if mid != 1.0:
+        direction, image = (every(lambda a: a / mid, f) for f in (direction, image))
     rho = 1.0 / ratio
     for step in range(ITERS):
         x = every(lambda a, b: a + b, x, direction)
-        residual = every(lambda a, b: a - b, residual, apply(direction))
+        if step == 0 and mid == 1.0:
+            residual = across(direction)
+        else:
+            residual = every(lambda r, m, c: (r - m) + c, residual, image, across(direction))
         if step + 1 < ITERS:
             rho_next = 1.0 / (2.0 * ratio - rho)
             keep, gain = rho_next * rho, 2.0 * rho_next / half
             direction = every(lambda d, z: keep * d + gain * z, direction, precondition(residual))
+            image = every(lambda m, r: keep * m + gain * r, image, residual)
             rho = rho_next
     squares = functools.reduce(lambda a, b: a + b, [a * a for a in residual[0]])
     share(jnp.sum(jnp.sum(squares, axis=1, keepdims=True), axis=0, keepdims=True))
@@ -719,8 +743,12 @@
 
 
 def finish_kernel(kept, x_ref, ot_ref, os_ref, ou_ref, ov_ref, ox_ref, orms_ref, rms, sem):
+    K = kept.shape[1]
+    piece = K // 4 if K % 4 == 0 else K
     for f, target in enumerate((ot_ref, os_ref, ou_ref, ov_ref)):
-        pltpu.make_async_copy(kept.at[f], target, sem.at[0]).start()
+        for first in range(0, K, piece):
+            levels = pl.ds(first, piece)
+            pltpu.make_async_copy(kept.at[f, levels], target.at[levels], sem.at[0]).start()
     surface = pltpu.make_async_copy(x_ref.at[0], ox_ref, sem.at[1])
     surface.start()
     rms[0] = jnp.max(x_ref[1])
@@ -755,8 +783,8 @@
             pack, pack, room(2, 2), room(2, 2), room(2), room(2), room(4),
             room(2, K), room(K), pltpu.VMEM((n_lon, TILES * NI, NJ), F32), room(2), room(2, n_lon), room(n_lat),
             pltpu.VMEM((3, n_lon * NI, NJ), F32),
-            pltpu.SemaphoreType.DMA((3,)), pltpu.SemaphoreType.DMA((3,)), pltpu.SemaphoreType.DMA((NC + 2,)),
-            pltpu.SemaphoreType.DMA((4,)), pltpu.SemaphoreType.DMA((4,)), pltpu.SemaphoreType.DMA((3, 3)),
+            pltpu.SemaphoreType.DMA((3,)), pltpu.SemaphoreType.DMA((3,)), pltpu.SemaphoreType.DMA((4,)),
+            pltpu.SemaphoreType.DMA((4,)), pltpu.SemaphoreType.DMA((4,)), pltpu.SemaphoreType.DMA((7,)),
         ],
         compiler_params=pltpu.CompilerParams(
             collective_id=0, has_side_effects=True),

time: 20.9 us -> 20.9 us (level)
  no operation moved by 1% of the time
where the time goes in v6:
time: 20.9 us; the launch traced here: 20.8 us
  Pallas kernels  20.1 us (96%)
  between operations  0.64 us (3%)
    pallas_call x1, Pallas kernels, per_device(): pl.pallas_call(functools.partial(step_kernel, n_lon, n_lat, KC), out_shap...  19.3 us
    pallas_call x1, Pallas kernels, per_device(): pl.pallas_call(finish_kernel, out_shape=(big, big, big, big, tile, one),...  0.81 us

profile of v6, /device:TPU:0, one launch (start us, length us, event | category | flops | bytes accessed | tf_op | source)
XLA Modules:
  0.0 20.8 jit_solution(294780241940365629)
XLA Ops:
  0.6 19.3 %step.1 = (f32[4,32,8,128]{3,2,1,0:T(8,128)S(1)}, f32[2,8,128]{2,1,0:T(8,128)S(1)}) custom-call(f32[32,8,128]{2,1,0:T(8,128)} %refs_0_.1, f32[32,8,128]{2,1,0:T(8,128)} %refs_1_.1, f32[32,8,128]{2,1,0:T(8,128)} %refs_2_.1, f32[32,8,128]{2,1,0:T(8,128)} %refs_3_.1, s32[8,128]{1,0:T(8,128)} %refs_4_.1, s32[8,128]{1,0:T(8,128)} %refs_5_.1, f32[32]{0:T(128)} %refs_6_.1, ...), custom_call_target="tpu_custom_call" | custom-call | tf_op jit(solution)/shard_map/step/pallas_call | solution.py:776
  19.9 0.8 %finish.1 = (f32[32,8,128]{2,1,0:T(8,128)}, f32[32,8,128]{2,1,0:T(8,128)}, f32[32,8,128]{2,1,0:T(8,128)}, f32[32,8,128]{2,1,0:T(8,128)}, f32[8,128]{1,0:T(8,128)}, /*index=5*/f32[1]{0:T(128)}) custom-call(f32[4,32,8,128]{3,2,1,0:T(8,128)S(1)} %get-tuple-element.14.kept, f32[2,8,128]{2,1,0:T(8,128)S(1)} %get-tuple-element.15.x_ref), custom_call_target="tpu_custom_call" | custom-call | tf_op jit(solution)/shard_map/finish/pallas_call | solution.py:793

commit v7 on v6

--- a/solution.py
+++ b/solution.py
@@ -271,13 +271,13 @@
             send(0, 0, p, p, q - 1, 1)
 
         def to(lon):
+            copy(mine, mine, lon, q, cast_send.at[0], cast_recv.at[3 * which]).start()
+
             @pl.when(not_south)
             def _():
                 send(0, 0, p, lon, q - 1, 1)
 
             send(1, side, slot, lon, lat, 2)
-            copy(mine, mine, lon, q, cast_send.at[0], cast_recv.at[3 * which]).start()
-
         each_other(to)
 
     def cast_wait(which):
@@ -491,9 +491,10 @@
 
     def share(total):
         sums[q] = jnp.broadcast_to(total, (NI, NJ))
+        mine = sums.at[q, pl.ds(0, 1)]
         for r in range(1, n_lat):
-            lat = lax.rem(q + r, n_lat)
-            copy(sums.at[q], sums.at[q], p, lat, cast_send.at[3], cast_recv.at[6]).start()
+            lat = jnp.where(r <= q, r - 1, r)
+            copy(mine, mine, p, lat, cast_send.at[3], cast_recv.at[6]).start()
 
 
     def late_wait():
@@ -609,10 +610,11 @@
     def _():
         drain(rims.at[0, pl.ds(0, n_lon - 1), used], cast_send.at[2])
 
-    drain(sums.at[pl.ds(0, n_lat - 1)], cast_recv.at[6])
-    total = functools.reduce(lambda a, b: a + b, [sums[lat] for lat in range(n_lat)])
-    ox_ref[1] = jnp.sqrt(total / (n_lon * NI * n_lat * NJ) + EPSILON)
-    drain(sums.at[pl.ds(0, n_lat - 1)], cast_send.at[3])
+    drain(sums.at[pl.ds(0, n_lat - 1), pl.ds(0, 1)], cast_recv.at[6])
+    total = functools.reduce(lambda a, b: a + b, [sums[lat, 0:1] for lat in range(n_lat)])
+    rms = jnp.sqrt(total / (n_lon * NI * n_lat * NJ) + EPSILON)
+    ox_ref[1] = jnp.broadcast_to(rms, (NI, NJ))
+    drain(sums.at[pl.ds(0, n_lat - 1), pl.ds(0, 1)], cast_send.at[3])
 
 
 def surface_solve(load, rim_rows, late_wait, share, n_lon, K, NI, NJ):

time: 20.9 us -> 20.8 us (level)
  no operation moved by 1% of the time
where the time goes in v7:
time: 20.8 us; the launch traced here: 20.6 us
  Pallas kernels  20 us (96%)
  between operations  0.64 us (3%)
    pallas_call x1, Pallas kernels, per_device(): pl.pallas_call(functools.partial(step_kernel, n_lon, n_lat, KC), out_shap...  19.1 us
    pallas_call x1, Pallas kernels, per_device(): pl.pallas_call(finish_kernel, out_shape=(big, big, big, big, tile, one),...  0.81 us

profile of v7, /device:TPU:0, one launch (start us, length us, event | category | flops | bytes accessed | tf_op | source)
XLA Modules:
  0.0 20.6 jit_solution(1304237360214746672)
XLA Ops:
  0.6 19.1 %step.1 = (f32[4,32,8,128]{3,2,1,0:T(8,128)S(1)}, f32[2,8,128]{2,1,0:T(8,128)S(1)}) custom-call(f32[32,8,128]{2,1,0:T(8,128)} %refs_0_.1, f32[32,8,128]{2,1,0:T(8,128)} %refs_1_.1, f32[32,8,128]{2,1,0:T(8,128)} %refs_2_.1, f32[32,8,128]{2,1,0:T(8,128)} %refs_3_.1, s32[8,128]{1,0:T(8,128)} %refs_4_.1, s32[8,128]{1,0:T(8,128)} %refs_5_.1, f32[32]{0:T(128)} %refs_6_.1, ...), custom_call_target="tpu_custom_call" | custom-call | tf_op jit(solution)/shard_map/step/pallas_call | solution.py:778
  19.8 0.8 %finish.1 = (f32[32,8,128]{2,1,0:T(8,128)}, f32[32,8,128]{2,1,0:T(8,128)}, f32[32,8,128]{2,1,0:T(8,128)}, f32[32,8,128]{2,1,0:T(8,128)}, f32[8,128]{1,0:T(8,128)}, /*index=5*/f32[1]{0:T(128)}) custom-call(f32[4,32,8,128]{3,2,1,0:T(8,128)S(1)} %get-tuple-element.14.kept, f32[2,8,128]{2,1,0:T(8,128)S(1)} %get-tuple-element.15.x_ref), custom_call_target="tpu_custom_call" | custom-call | tf_op jit(solution)/shard_map/finish/pallas_call | solution.py:795

commit v8 on v7

--- a/solution.py
+++ b/solution.py
@@ -737,7 +737,10 @@
             direction = every(lambda d, z: keep * d + gain * z, direction, precondition(residual))
             image = every(lambda m, r: keep * m + gain * r, image, residual)
             rho = rho_next
-    squares = functools.reduce(lambda a, b: a + b, [a * a for a in residual[0]])
+    squares = [a * a for a in residual[0]]
+    while len(squares) > 1:
+        squares = [a + b for a, b in zip(squares[::2], squares[1::2])] + squares[len(squares) & ~1:]
+    squares = squares[0]
     share(jnp.sum(jnp.sum(squares, axis=1, keepdims=True), axis=0, keepdims=True))
     slope_x = every(lambda e, w: 0.5 * (e - w), east(x), west(x))
     slope_y = every(lambda n, s: 0.5 * (n - s), north(x), south(x))

time: 20.8 us -> 20.8 us (level)
  no operation moved by 1% of the time
where the time goes in v8:
time: 20.8 us; the launch traced here: 20.6 us
  Pallas kernels  20 us (96%)
  between operations  0.64 us (3%)
    pallas_call x1, Pallas kernels, per_device(): pl.pallas_call(functools.partial(step_kernel, n_lon, n_lat, KC), out_shap...  19.1 us
    pallas_call x1, Pallas kernels, per_device(): pl.pallas_call(finish_kernel, out_shape=(big, big, big, big, tile, one),...  0.81 us

profile of v8, /device:TPU:0, one launch (start us, length us, event | category | flops | bytes accessed | tf_op | source)
XLA Modules:
  0.0 20.6 jit_solution(9705370487264054827)
XLA Ops:
  0.6 19.1 %step.1 = (f32[4,32,8,128]{3,2,1,0:T(8,128)S(1)}, f32[2,8,128]{2,1,0:T(8,128)S(1)}) custom-call(f32[32,8,128]{2,1,0:T(8,128)} %refs_0_.1, f32[32,8,128]{2,1,0:T(8,128)} %refs_1_.1, f32[32,8,128]{2,1,0:T(8,128)} %refs_2_.1, f32[32,8,128]{2,1,0:T(8,128)} %refs_3_.1, s32[8,128]{1,0:T(8,128)} %refs_4_.1, s32[8,128]{1,0:T(8,128)} %refs_5_.1, f32[32]{0:T(128)} %refs_6_.1, ...), custom_call_target="tpu_custom_call" | custom-call | tf_op jit(solution)/shard_map/step/pallas_call | solution.py:781
  19.8 0.8 %finish.1 = (f32[32,8,128]{2,1,0:T(8,128)}, f32[32,8,128]{2,1,0:T(8,128)}, f32[32,8,128]{2,1,0:T(8,128)}, f32[32,8,128]{2,1,0:T(8,128)}, f32[8,128]{1,0:T(8,128)}, /*index=5*/f32[1]{0:T(128)}) custom-call(f32[4,32,8,128]{3,2,1,0:T(8,128)S(1)} %get-tuple-element.14.kept, f32[2,8,128]{2,1,0:T(8,128)S(1)} %get-tuple-element.15.x_ref), custom_call_target="tpu_custom_call" | custom-call | tf_op jit(solution)/shard_map/finish/pallas_call | solution.py:798

commit v9 on v8

--- a/solution.py
+++ b/solution.py
@@ -362,7 +362,6 @@
     rim[1] = ps0
 
     drain(pack_in.at[:, bounds[0][0]:bounds[0][1]], chunk_sem.at[0])
-    sides(REST, 2 * K, 2)
     base_e = pack_in[0, 0:1, :]
     base_w = pack_in[1, 0:1, :]
     is_w = sub == 0
@@ -440,6 +439,7 @@
     pack_strips(1, -1.0, (*totals, out_rows), ns_rows)
     cast(1)
 
+    sides(REST, 2 * K, 2)
     for side, (d, push) in enumerate(((NI - 1, 0.5 * PRESSURE_SCALE), (0, -0.5 * PRESSURE_SCALE))):
         row = REST + 2 * K
         pack_out[side, row:row + K, :] = push * pressure[:, d, :] - FRICTION * laps[0, :, d, :]

time: 20.8 us -> 20.8 us (level)
  no operation moved by 1% of the time
where the time goes in v9:
time: 20.8 us; the launch traced here: 20.6 us
  Pallas kernels  19.9 us (96%)
  between operations  0.64 us (3%)
    pallas_call x1, Pallas kernels, per_device(): pl.pallas_call(functools.partial(step_kernel, n_lon, n_lat, KC), out_shap...  19.1 us
    pallas_call x1, Pallas kernels, per_device(): pl.pallas_call(finish_kernel, out_shape=(big, big, big, big, tile, one),...  0.81 us

profile of v9, /device:TPU:0, one launch (start us, length us, event | category | flops | bytes accessed | tf_op | source)
XLA Modules:
  0.0 20.6 jit_solution(10233959767283118924)
XLA Ops:
  0.6 19.1 %step.1 = (f32[4,32,8,128]{3,2,1,0:T(8,128)S(1)}, f32[2,8,128]{2,1,0:T(8,128)S(1)}) custom-call(f32[32,8,128]{2,1,0:T(8,128)} %refs_0_.1, f32[32,8,128]{2,1,0:T(8,128)} %refs_1_.1, f32[32,8,128]{2,1,0:T(8,128)} %refs_2_.1, f32[32,8,128]{2,1,0:T(8,128)} %refs_3_.1, s32[8,128]{1,0:T(8,128)} %refs_4_.1, s32[8,128]{1,0:T(8,128)} %refs_5_.1, f32[32]{0:T(128)} %refs_6_.1, ...), custom_call_target="tpu_custom_call" | custom-call | tf_op jit(solution)/shard_map/step/pallas_call | solution.py:781
  19.8 0.8 %finish.1 = (f32[32,8,128]{2,1,0:T(8,128)}, f32[32,8,128]{2,1,0:T(8,128)}, f32[32,8,128]{2,1,0:T(8,128)}, f32[32,8,128]{2,1,0:T(8,128)}, f32[8,128]{1,0:T(8,128)}, /*index=5*/f32[1]{0:T(128)}) custom-call(f32[4,32,8,128]{3,2,1,0:T(8,128)S(1)} %get-tuple-element.14.kept, f32[2,8,128]{2,1,0:T(8,128)S(1)} %get-tuple-element.15.x_ref), custom_call_target="tpu_custom_call" | custom-call | tf_op jit(solution)/shard_map/finish/pallas_call | solution.py:798
